TPU v7x, 32 devices: a whole 2x2x4 slice. The times are simulated.
32 devices in a mesh: grp: 4 (over y, x), node: 8 (over z, core).
Axes of the slice: x: 2, y: 2, z: 4, core: 2. Of those that a mesh axis runs over, the one named last changes fastest.
Arguments:
- damage: bfloat16 [1024, 16384], P('grp', 'node'), may hold values from -6 to 6
- basis_table: bfloat16 [1024, 512], P('grp'), may hold values from -6 to 6
- train_ids: int32 [1024], P('grp'), may hold values from 0 to 1023, each once
- counts: int32 [4], replicated, may hold values from 64 to 256
- new_table: bfloat16 [512, 512], replicated, may hold values from -6 to 6
- new_ids: int32 [256], replicated, may hold values from 0 to 511
Outputs:
- surrogate: bfloat16 [256, 16384], P('grp', 'node')
- peak: float32 [256], P('grp')
- spread: float32 [256], P('grp')
Inputs may be any that keep to these rules, and one draw needn't show every extreme that they name: `train_ids`: each row of basis_table is named by exactly one slot.
All inputs are finite; a program needn't handle non-finite values.
Results may differ from a plain program's by a relative error of at most 0.0085.
Values may be sent and summed in bfloat16 or wider, within the bound.
No kernel may reach another device: no remote copies, remote signals or barrier semaphores. Data moves between devices by JAX's collectives and lax.ppermute only.
A program may use at most 64 MiB of HBM per device.

v0:
```python
import jax
import jax.numpy as jnp
from jax import lax
from jax.sharding import PartitionSpec as P


def joined(value, axis, combine):
    everything = jax.tree.map(lambda part: lax.all_gather(part, axis), value)
    leading = jax.tree.map(lambda part: part[0], everything)

    def hop(k, so_far):
        return combine(so_far, jax.tree.map(lambda part: part[k], everything))

    return lax.fori_loop(1, lax.axis_size(axis), hop, leading)


def combine_stats(first, second):
    return (first[0] + second[0], jnp.maximum(first[1], second[1]))


def local(damage, basis_table, train_ids, counts, new_table, new_ids):
    slot_count = damage.shape[0]
    node_cells = damage.shape[1]
    group_index = lax.axis_index("grp")
    group_total = lax.axis_size("grp")
    total_nodes = node_cells * lax.axis_size("node")
    per_group = new_ids.shape[0] // group_total
    sample_total = jnp.sum(counts).astype(jnp.float32)
    basis_whole, ids_whole = (
        lax.all_gather(basis_table, "grp", axis=0, tiled=True),
        lax.all_gather(train_ids, "grp", axis=0, tiled=True),
    )
    my_slot_ids = lax.dynamic_slice_in_dim(ids_whole, group_index * slot_count, slot_count, 0)
    live_slot = jnp.arange(slot_count, dtype=jnp.int32) < counts[group_index]
    chosen = jnp.take(basis_whole, my_slot_ids, axis=0)
    weighted = jnp.where(live_slot[:, None], chosen, jnp.zeros_like(chosen))
    my_ids = lax.dynamic_slice_in_dim(new_ids, group_index * per_group, per_group, 0)
    new_rows = jnp.take(new_table, my_ids, axis=0)
    term_cols = weighted
    product = lax.dot_general(
        term_cols, damage, (((0,), (0,)), ((), ())), preferred_element_type=jnp.float32
    )
    coef_share = lax.psum_scatter(product / sample_total, "grp", scatter_dimension=0, tiled=True)
    term_cols = new_rows
    values = jnp.dot(
        term_cols,
        lax.all_gather(coef_share.astype(jnp.bfloat16), "grp", axis=0, tiled=True),
        preferred_element_type=jnp.float32,
    )
    local_square = jnp.sum(values * values, axis=1)
    local_peak = jnp.max(values, axis=1)
    squares, peak_value = joined((local_square, local_peak), "node", combine_stats)
    surrogate = values.astype(jnp.bfloat16)
    spread = jnp.sqrt(squares / total_nodes + 1e-06)
    return (surrogate, peak_value, spread)


def solution(mesh):
    placed = (P("grp", "node"), P("grp", None), P("grp"), P(), P(), P())
    return jax.shard_map(
        local,
        mesh=mesh,
        in_specs=placed,
        out_specs=(P("grp", "node"), P("grp"), P("grp")),
        check_vma=False,
    )
```

profile of v0, /device:TPU:0, one launch (start us, length us, event | category | flops | bytes accessed | tf_op | source)
XLA Modules:
  0.0 161.7 jit_solution(1231558724220339000)
XLA Ops:
  7.2 0.0 copy-start
  7.2 0.0 all-gather.6.cloned.1.call-start
  7.2 0.7 all-gather.6.cloned.1.call-update
  7.9 0.0 reduce-scatter.2.cloned.1.call-start
  8.0 1.3 reduce_sum.18
  9.3 1.2 dynamic_slice.30
  11.1 9.7 %all-gather.2 = s32[4,1,256]{2,1,0:T(1,128)S(1)} all-gather(s32[1,1,256]{2,1,0:T(1,128)} %bitcast.13), channel_id=1, replica_groups=mesh['grp'=4,'node'=8] {'grp'}, dimensions={0}, use_global_device_ids=true | all-gather | bytes 5120 | tf_op jit(solution)/shard_map/all_gather | solution.py:31
  20.8 0.7 compare_and_fusion
  21.6 17.5 %all-gather.6.cloned.1.call-done = bf16[1024,512]{1,0:T(8,128)(2,1)} async-done(((bf16[256,512]{1,0:T(8,128)(2,1)}), bf16[1024,512]{1,0:T(8,128)(2,1)}) %all-gather.6.cloned.1.call-update) | async-done | bytes 1048592 | tf_op jit(solution)/shard_map/all_gather | solution.py:30
  39.1 2.6 %gather_fusion.1 = bf16[256,512]{1,0:T(8,128)(2,1)S(1)} fusion(bf16[1024,512]{1,0:T(8,128)(2,1)} %all-gather.6.cloned.1.call-done, s32[1024]{0:T(1024)S(1)} %pad_clamp_fusion), kind=kCustom, calls=%fused_computation.1 | custom fusion | bytes 525312 | tf_op jit(solution)/shard_map/jit(_take)/gather | solution.py:35
  41.7 0.0 copy-done
  41.7 2.8 %convolution_divide_fusion = f32[512,2048]{1,0:T(8,128)} fusion(bf16[256,2048]{1,0:T(8,128)(2,1)S(1)} %copy-done, f32[]{:T(128)S(6)} %convert_element_type.9, bf16[256,512]{1,0:T(8,128)(2,1)S(1)} %gather_fusion.1, pred[256]{0:T(512)(128)(4,1)S(1)} %get-tuple-element.154, pred[256]{0:T(512)(128)(4,1)S(1)} %get-tuple-element.160), kind=kOutput, calls=%fused_computation.4 | convolution fusion | flops 538181632 | bytes 5505540 | tf_op jit(solution)/shard_map/dot_general | solution.py:40
  44.5 0.0 copy-start.3
  44.5 0.0 copy-start.1
  44.5 0.0 copy-start.4
  44.5 0.0 reduce-scatter.2.cloned.1.call-update
  44.5 0.0 all-gather.8.cloned.1.call-start
  44.6 52.7 %reduce-scatter.2.cloned.1.call-done = f32[128,2048]{1,0:T(8,128)} async-done(((f32[512,2048]{1,0:T(8,128)}), f32[128,2048]{1,0:T(8,128)}) %reduce-scatter.2.cloned.1.call-update) | async-done | bytes 1048592 | tf_op jit(solution)/shard_map/reduce_scatter | solution.py:43
  97.3 2.1 %convert_element_type.10 = bf16[128,2048]{1,0:T(8,128)(2,1)} convert(f32[128,2048]{1,0:T(8,128)} %reduce-scatter.2.cloned.1.call-done) | non-fusion elementwise | flops 262144 | bytes 1572864 | tf_op jit(solution)/shard_map/convert_element_type | solution.py:47
  99.3 0.0 all-gather.8.cloned.1.call-update
  99.4 0.0 copy-done.3
  99.4 0.1 compare_and_fusion.1
  99.5 0.0 copy-done.1
  99.5 0.7 gather_fusion
  100.2 0.0 copy-done.4
  100.2 0.6 dynamic-slice
  101.4 33.3 %all-gather.8.cloned.1.call-done = bf16[512,2048]{1,0:T(8,128)(2,1)} async-done(((bf16[128,2048]{1,0:T(8,128)(2,1)}), bf16[512,2048]{1,0:T(8,128)(2,1)}) %all-gather.8.cloned.1.call-update) | async-done | bytes 2097168 | tf_op jit(solution)/shard_map/all_gather | solution.py:47
  134.7 2.9 %fusion.13 = (f32[64]{0:T(128)S(1)}, f32[64]{0:T(128)S(1)}, bf16[64,2048]{1,0:T(8,128)(2,1)}) fusion(bf16[512,2048]{1,0:T(8,128)(2,1)} %all-gather.8.cloned.1.call-done, bf16[64,512]{1,0:T(8,128)(2,1)S(1)} %gather_fusion, pred[64]{0:T(512)(128)(4,1)S(1)} %get-tuple-element.152), kind=kOutput, calls=%fused_computation.27 | convolution fusion | flops 134774656 | bytes 2425408 | tf_op jit(solution)/shard_map/dot_general | solution.py:45
  137.6 0.2 dynamic-update-slice
  137.9 0.2 dynamic-update-slice.1
  138.1 16.2 %all-reduce.2 = (f32[512]{0:T(512)S(1)}, f32[512]{0:T(512)S(1)}) all-reduce(f32[512]{0:T(512)S(1)} %dynamic-update-slice, f32[512]{0:T(512)S(1)} %dynamic-update-slice.1), channel_id=2, replica_groups=mesh['grp'=4,'node'=8] {'node'}, use_global_device_ids=true, to_apply=%add | all-reduce | flops 1024 | bytes 8192
  154.2 0.1 reshape.36
  154.3 0.1 reshape.37
  154.4 0.2 while.17
  154.7 0.0 copy-start.2
  154.7 0.5 add_sqrt_fusion
  155.2 0.0 copy-done.2
  (13 shorter events, 0.1 us)
Async XLA Ops:
  7.2 34.5 %copy-start = (bf16[256,2048]{1,0:T(8,128)(2,1)S(1)}, bf16[256,2048]{1,0:T(8,128)(2,1)}, u32[]{:S(2)}) copy-start(bf16[256,2048]{1,0:T(8,128)(2,1)} %param.8) | copy-start | bytes 3145732
  7.2 31.9 %all-gather.6.cloned.1.call-start = ((), (), s32[]{:S(2)}) async-start(), calls=%async_computation.1 | async-start | bytes 1310720 | tf_op jit(solution)/shard_map/all_gather | solution.py:30
  7.9 89.3 %reduce-scatter.2.cloned.1.call-start = ((), (), s32[]{:S(2)}) async-start(), calls=%async_computation.2 | async-start | bytes 5242880 | tf_op jit(solution)/shard_map/reduce_scatter | solution.py:43
  44.5 54.9 %copy-start.3 = (s32[256]{0:T(256)S(1)}, s32[256]{0:T(256)}, u32[]{:S(2)}) copy-start(s32[256]{0:T(256)} %param.13) | copy-start | bytes 3076
  44.5 55.0 %copy-start.1 = (bf16[512,512]{1,0:T(8,128)(2,1)S(1)}, bf16[512,512]{1,0:T(8,128)(2,1)}, u32[]{:S(2)}) copy-start(bf16[512,512]{1,0:T(8,128)(2,1)} %param.12) | copy-start | bytes 1572868
  44.5 55.7 %copy-start.4 = (u32[32]{0:T(128)S(1)}, u32[32]{0:T(128)}, u32[]{:S(2)}) copy-start(u32[32]{0:T(128)} %constant.92) | copy-start | bytes 388
  44.5 90.2 %all-gather.8.cloned.1.call-start = ((), (), s32[]{:S(2)}) async-start(), calls=%async_computation.3 | async-start | bytes 2621440 | tf_op jit(solution)/shard_map/all_gather | solution.py:47
  154.7 0.5 copy-start.2
Sparse Core Ops, SparseCore 0:
  9.8 29.2 all-gather.5
  44.6 52.5 reduce-scatter.1
  99.5 35.1 all-gather.7
where the time goes:
time: 162 us
  waiting for transfers between devices  104 us (64%)
  blocking collectives  25.9 us (16%)
  between operations  15.1 us (9%)
  local copies, waits for them, and re-layouts  5.73 us (4%)
  matrix products  5.73 us (4%)
  other arithmetic  4.84 us (3%)
    reduce_scatter x1, waiting for transfers between devices, local(): lax.psum_scatter(product / sample_total, 'grp', scatter_dimension=0, tile...  52.7 us
    all_gather x1, waiting for transfers between devices, local(): lax.all_gather(coef_share.astype(jnp.bfloat16), 'grp', axis=0, tiled=True)  33.3 us
    all_gather x1, waiting for transfers between devices, local(): lax.all_gather(basis_table, 'grp', axis=0, tiled=True)  17.5 us
    unnamed x1, blocking collectives  16.2 us
    all_gather x1, blocking collectives, local(): lax.all_gather(train_ids, 'grp', axis=0, tiled=True)  9.7 us
  transfers between devices with their start and end apart: 3, of which 3 were waited for; matrix products, arithmetic and copies ran while one was open for 3% of the time, Pallas kernels for 0%

commit v1 on v0

v1 whole, which is shorter than its diff:
```python
import functools

import jax
import jax.numpy as jnp
from jax import lax
from jax.experimental import pallas as pl
from jax.experimental.pallas import tpu as pltpu
from jax.sharding import PartitionSpec as P


FULL = pl.BlockSpec(memory_space=pltpu.VMEM)
FAR = pl.BlockSpec(memory_space=pltpu.HBM)


def mate(index, step, size):
    return index ^ step if size & (size - 1) == 0 else (index + step) % size


def origin(index, step, size):
    return index ^ step if size & (size - 1) == 0 else (index - step) % size


def swap(value, axis, step):
    size = lax.axis_size(axis)
    return lax.ppermute(value, axis, [(i, mate(i, step, size)) for i in range(size)])


def split_swap(value, steps):
    nodes = lax.axis_size("node")
    pairs = [
        (group * nodes + node, (group ^ steps[node % 2]) * nodes + node)
        for group in range(lax.axis_size("grp"))
        for node in range(nodes)
    ]
    return lax.ppermute(value, ("grp", "node"), pairs)


def params(size):
    return pltpu.CompilerParams(vmem_limit_bytes=size)


def cost(flops):
    return pl.CostEstimate(flops=flops, bytes_accessed=1 << 20, transcendentals=0)


def scores_kernel(groups, table_ref, ids_ref, basis_ref, train_ref, counts_ref, damage_ref, *refs):
    scores, half, named, damage, table, ids, basis, train, counts, choice, sems = refs
    pairs = (
        (counts_ref, counts),
        (ids_ref, ids),
        (train_ref, train),
        (table_ref, table),
        (basis_ref, basis),
        (damage_ref, damage),
    )
    copies = [pltpu.make_async_copy(src, dst, sems.at[k]) for k, (src, dst) in enumerate(pairs)]
    for copy in copies:
        copy.start()
    me = lax.axis_index("grp")
    samples = ids.shape[1]
    copies[1].wait()
    lane = lax.broadcasted_iota(jnp.int32, (samples, 128), 1)
    wanted = jnp.transpose(jnp.broadcast_to(ids[...].astype(jnp.float32), (128, samples)))
    for start in range(0, table.shape[0], 128):
        match = wanted == (lane + start).astype(jnp.float32)
        choice[:, start : start + 128] = match.astype(jnp.bfloat16)
    copies[0].wait()
    total = lax.fori_loop(0, groups, lambda k, s: s + counts[k], jnp.int32(0)).astype(jnp.float32)
    copies[3].wait()
    chosen = jnp.dot(choice[...], table[...], preferred_element_type=jnp.float32)
    copies[4].wait()
    found = lax.dot_general(
        chosen.astype(jnp.bfloat16),
        basis[...],
        (((1,), (1,)), ((), ())),
        preferred_element_type=jnp.float32,
    )
    scores[...] = (found / total).astype(jnp.bfloat16)
    rows = half.shape[0]
    odd = lax.axis_index("node") % 2
    half[...] = scores[pl.ds(pl.multiple_of(odd * rows, rows), rows), :]
    copies[2].wait()
    live = lax.broadcasted_iota(jnp.int32, named.shape, 1) < counts[me]
    named[...] = jnp.where(live, train[...], -1)
    copies[5].wait()


def picks_kernel(groups, named_ref, out_ref):
    me = lax.axis_index("grp")
    row = lax.broadcasted_iota(jnp.int32, out_ref.shape[1:], 0)
    for step in range(groups):
        first = origin(me, step, groups) * out_ref.shape[1]
        out_ref[step] = jnp.where(row == named_ref[...] - first, 1.0, 0.0).astype(out_ref.dtype)


def targets(paired, groups):
    if paired:
        odd = lax.axis_index("node") % 2
        return 3, [1 + odd], [2 - odd]
    return groups - 1, list(range(1, groups - 1)), []


def blocks(paired, groups, refs):
    if not paired:
        return [(refs[step], step) for step in range(groups)]
    own, near, mated, half, other, joined = refs
    odd = lax.axis_index("node") % 2
    rows = half.shape[0]
    joined[pl.ds(pl.multiple_of(odd * rows, rows), rows), :] = half[...]
    joined[pl.ds(pl.multiple_of((1 - odd) * rows, rows), rows), :] = other[...]
    return [(own, 0), (near, 1 + odd), (mated, 2 - odd), (joined, 3)]


def weights(groups, per_group, wanted, picks_ref, found, order_ref):
    me = lax.axis_index("grp")
    total = None
    for ref, step in found:
        for place, target in enumerate(wanted):
            first = pl.multiple_of(mate(me, target, groups) * per_group, per_group)
            order_ref[place * per_group : (place + 1) * per_group, :] = ref[pl.ds(first, per_group), :]
        part = jnp.dot(
            order_ref[: len(wanted) * per_group, :],
            picks_ref[step],
            preferred_element_type=jnp.float32,
        )
        total = part if total is None else total + part
    return total.astype(jnp.bfloat16)


def project(weight, damage_ref, outs, tile):
    rows = weight.shape[0] // len(outs)
    for start in range(0, damage_ref.shape[1], tile):
        part = jnp.dot(
            weight, damage_ref[:, start : start + tile], preferred_element_type=jnp.float32
        )
        for k, pieces in enumerate(outs):
            width = pieces[0].shape[1]
            out, at = pieces[start // width], start % width
            out[:, at : at + tile] = part[k * rows : (k + 1) * rows, :].astype(out.dtype)


def first_kernel(paired, groups, per_group, tile, picks_ref, damage_ref, *refs):
    refs, order = list(refs[:-1]), refs[-1]
    joined = [refs.pop()] if paired else []
    pieces = 2 if paired else 1
    scores, outs = refs[:-pieces], refs[-pieces:]
    first, _, _ = targets(paired, groups)
    found = blocks(paired, groups, scores + joined)
    weight = weights(groups, per_group, [first], picks_ref, found, order)
    project(weight, damage_ref, [outs], tile)


def other_kernel(paired, groups, per_group, tile, picks_ref, damage_ref, *refs):
    refs, order = list(refs[:-1]), refs[-1]
    joined = [refs.pop()] if paired else []
    _, sent, kept = targets(paired, groups)
    count = len(sent) + 2 * len(kept)
    scores, outs, own = refs[: -count - 1], refs[-count - 1 : -1], refs[-1]
    found = blocks(paired, groups, scores + joined)
    weight = weights(groups, per_group, sent + kept + [0], picks_ref, found, order)
    rows = (len(sent) + len(kept)) * per_group
    own[...] = weight[rows:, :]
    outs = [[out] for out in outs[: len(sent)]] + ([outs[len(sent) :]] if kept else [])
    project(weight[:rows, :], damage_ref, outs, tile)


def own_kernel(tile, weight_ref, damage_ref, out_ref):
    project(weight_ref[...], damage_ref, [[out_ref]], tile)


def add_kernel(one_ref, two_ref, out_ref):
    out_ref[...] = (one_ref[...] + two_ref[...].astype(jnp.float32)).astype(out_ref.dtype)


def values_kernel(own_ref, *refs):
    parts, (out_ref, stats_ref) = refs[:-2], refs[-2:]
    rows, cells = out_ref.shape
    square = peak = None
    width = min(part.shape[1] for part in parts)
    for start in range(0, cells, width):
        values = own_ref[:, start : start + width]
        place = 0
        for part in parts:
            if place <= start < place + part.shape[1]:
                values = values + part[:, start - place : start - place + width].astype(jnp.float32)
            place = (place + part.shape[1]) % cells
        out_ref[:, start : start + width] = values
        more = jnp.sum(values * values, axis=1, keepdims=True)
        high = jnp.max(values, axis=1, keepdims=True)
        square = more if square is None else square + more
        peak = high if peak is None else jnp.maximum(peak, high)
    stats_ref[0:1, :] = jnp.transpose(jnp.broadcast_to(square, (rows, 128)))[0:1, :]
    stats_ref[1:2, :] = jnp.transpose(jnp.broadcast_to(peak, (rows, 128)))[0:1, :]


def round_kernel(values_ref, out_ref):
    out_ref[...] = values_ref[...].astype(out_ref.dtype)


def combine(first, second):
    return jnp.stack([first[0] + second[0], jnp.maximum(first[1], second[1])])


def over_nodes(stats, nodes):
    if nodes & (nodes - 1):
        everything = lax.all_gather(stats, "node")
        return jnp.stack([jnp.sum(everything[:, 0], axis=0), jnp.max(everything[:, 1], axis=0)])
    step = 1
    while step < nodes:
        stats = combine(stats, swap(stats, "node", step))
        step *= 2
    return stats


def local(damage, basis_table, train_ids, counts, new_table, new_ids):
    slots, cells = damage.shape
    groups = lax.axis_size("grp")
    nodes = lax.axis_size("node")
    samples = new_ids.shape[0]
    per_group = samples // groups
    rows = basis_table.shape[0]
    half = jnp.bfloat16
    paired = groups == 4 and nodes % 2 == 0

    far = [
        pltpu.with_memory_space_constraint(x, pltpu.HBM)
        for x in (
            new_table,
            new_ids.reshape(1, samples),
            basis_table,
            train_ids.reshape(1, slots),
            counts,
            damage,
        )
    ]
    scores, own_half, named, damage = pl.pallas_call(
        functools.partial(scores_kernel, groups),
        out_shape=[
            jax.ShapeDtypeStruct((samples, rows), half),
            jax.ShapeDtypeStruct((samples // 2, rows), half),
            jax.ShapeDtypeStruct((1, slots), jnp.int32),
            jax.ShapeDtypeStruct((slots, cells), half),
        ],
        in_specs=[FAR] * 6,
        out_specs=[FULL] * 4,
        scratch_shapes=[
            pltpu.VMEM(new_table.shape, half),
            pltpu.VMEM((1, samples), jnp.int32),
            pltpu.VMEM(basis_table.shape, half),
            pltpu.VMEM((1, slots), jnp.int32),
            pltpu.SMEM((groups,), jnp.int32),
            pltpu.VMEM((samples, new_table.shape[0]), half),
            pltpu.SemaphoreType.DMA((6,)),
        ],
        compiler_params=params(32 << 20),
        name="scores",
    )(*far)

    picks = pl.pallas_call(
        functools.partial(picks_kernel, groups),
        out_shape=jax.ShapeDtypeStruct((groups, rows, slots), half),
        in_specs=[FULL],
        out_specs=FULL,
        compiler_params=params(16 << 20),
        cost_estimate=cost(1 << 20),
        name="picks",
    )(named)

    if paired:
        opposite = swap(own_half, "grp", 3)
        near = split_swap(scores, (1, 2))
        every = [scores, near, swap(near, "node", 1), opposite, swap(opposite, "node", 1)]
        width = cells // 2
        kinds = [(cells, half)] + [(width, jnp.float32)] * 2
        joined = [pltpu.VMEM((samples, rows), half)]
    else:
        every = [scores] + [swap(scores, "grp", step) for step in range(1, groups)]
        width = cells
        kinds = [(cells, half)] * (groups - 2)
        joined = []
    tile = min(width, 512)

    first = pl.pallas_call(
        functools.partial(first_kernel, paired, groups, per_group, tile),
        out_shape=[jax.ShapeDtypeStruct((per_group, width), half)] * (cells // width),
        in_specs=[FULL] * (2 + len(every)),
        out_specs=[FULL] * (cells // width),
        scratch_shapes=joined + [pltpu.VMEM((per_group, rows), half)],
        compiler_params=params(24 << 20),
        cost_estimate=cost(1 << 20),
        name="first",
    )(picks, damage, *every)
    if paired:
        passed = [split_swap(part, (1, 2)) for part in first]
    else:
        arrived = [swap(first[0], "grp", groups - 1)]

    wanted = 3 if paired else groups - 1
    *made, own_weight = pl.pallas_call(
        functools.partial(other_kernel, paired, groups, per_group, tile),
        out_shape=[jax.ShapeDtypeStruct((per_group, size), kind) for size, kind in kinds]
        + [jax.ShapeDtypeStruct((per_group, slots), half)],
        in_specs=[FULL] * (2 + len(every)),
        out_specs=[FULL] * (len(kinds) + 1),
        scratch_shapes=joined + [pltpu.VMEM((wanted * per_group, rows), half)],
        compiler_params=params(32 << 20),
        cost_estimate=cost(1 << 20),
        name="other",
    )(picks, damage, *every)
    if paired:
        add = pl.pallas_call(
            add_kernel,
            out_shape=jax.ShapeDtypeStruct((per_group, width), half),
            in_specs=[FULL] * 2,
            out_specs=FULL,
            compiler_params=params(16 << 20),
            cost_estimate=cost(1 << 20),
            name="add",
        )
        arrived = [split_swap(made[0], (1, 2))] + [
            split_swap(add(made[1 + k], passed[k]), (2, 1)) for k in range(2)
        ]
    else:
        arrived += [swap(part, "grp", step) for step, part in enumerate(made, 1)]

    own = pl.pallas_call(
        functools.partial(own_kernel, tile),
        out_shape=jax.ShapeDtypeStruct((per_group, cells), jnp.float32),
        in_specs=[FULL, FULL],
        out_specs=FULL,
        compiler_params=params(24 << 20),
        cost_estimate=cost(1 << 20),
        name="own",
    )(own_weight, damage)

    values, stats = pl.pallas_call(
        values_kernel,
        out_shape=[
            jax.ShapeDtypeStruct((per_group, cells), jnp.float32),
            jax.ShapeDtypeStruct((2, per_group), jnp.float32),
        ],
        in_specs=[FULL] * (1 + len(arrived)),
        out_specs=[FULL, FULL],
        compiler_params=params(24 << 20),
        name="values",
    )(own, *arrived)
    surrogate = pl.pallas_call(
        round_kernel,
        out_shape=jax.ShapeDtypeStruct((per_group, cells), half),
        in_specs=[FULL],
        out_specs=FULL,
        compiler_params=params(16 << 20),
        cost_estimate=cost(1 << 20),
        name="round",
    )(values)

    squares, peak = over_nodes(stats, nodes)
    spread = jnp.sqrt(squares / (cells * nodes) + 1e-06)
    return (surrogate, peak, spread)


def solution(mesh):
    placed = (P("grp", "node"), P("grp", None), P("grp"), P(), P(), P())
    return jax.shard_map(
        local,
        mesh=mesh,
        in_specs=placed,
        out_specs=(P("grp", "node"), P("grp"), P("grp")),
        check_vma=False,
    )
```

time: 162 us -> 35.1 us (0.22)
  waiting for transfers between devices: 104 us -> 14.7 us
  blocking collectives: 25.9 us -> 0 us
  starting transfers between devices: 0.12 us -> 14.6 us
  between operations: 15.1 us -> 0.68 us
  matrix products: 5.73 us -> 0 us
  local copies, waits for them, and re-layouts: 5.73 us -> 0 us
  Pallas kernels: 0 us -> 4.51 us
  other arithmetic: 4.84 us -> 0.56 us
    reduce_scatter x1 -> x0, waiting for transfers between devices: 52.7 us -> none  [local(): lax.psum_scatter(product / sample_total, 'grp', scatter_dimension=0, tile...]
    all_gather x2 -> x0, waiting for transfers between devices: 50.8 us -> none  [the longest x1 33.3 us: local(): lax.all_gather(coef_share.astype(jnp.bfloat16), 'grp', axis=0, tiled=True)]
    unnamed x1 -> x0, blocking collectives: 16.2 us -> none
    ppermute x0 -> x12, waiting for transfers between devices: none -> 14.7 us  [the longest x6 7.38 us: split_swap(): return lax.ppermute(value, ('grp', 'node'), pairs)]
    ppermute x0 -> x12, starting transfers between devices: none -> 14.6 us  [the longest x6 8.41 us: split_swap(): return lax.ppermute(value, ('grp', 'node'), pairs)]
    all_gather x1 -> x0, blocking collectives: 9.7 us -> none  [local(): lax.all_gather(train_ids, 'grp', axis=0, tiled=True)]
    dot_general x2 -> x0, matrix products: 5.73 us -> none  [the longest x1 2.93 us: local(): jnp.dot(term_cols, lax.all_gather(coef_share.astype(jnp.bfloat16), 'grp',...]
    pallas_call x0 -> x9, Pallas kernels: none -> 4.51 us  [the longest x1 1.84 us: local(): pl.pallas_call(functools.partial(scores_kernel, groups), out_shape=[jax.S...]
  transfers between devices with their start and end apart: 3 -> 12, of which waited for: 3 -> 10; matrix products, arithmetic and copies ran while one was open for 3% -> 0% of each run, Pallas kernels for 0% -> 5%
where the time goes in v1:
time: 35.1 us; the launch traced here: 35 us
  waiting for transfers between devices  14.7 us (42%)
  starting transfers between devices  14.6 us (42%)
  Pallas kernels  4.51 us (13%)
  between operations  0.68 us (2%)
  other arithmetic  0.56 us (2%)
    ppermute x6, starting transfers between devices, split_swap(): return lax.ppermute(value, ('grp', 'node'), pairs)  8.41 us
    ppermute x6, waiting for transfers between devices, split_swap(): return lax.ppermute(value, ('grp', 'node'), pairs)  7.38 us
    ppermute x6, waiting for transfers between devices, swap(): lax.ppermute(value, axis, [(i, mate(i, step, size)) for i in range(size)])  7.3 us
    ppermute x6, starting transfers between devices, swap(): lax.ppermute(value, axis, [(i, mate(i, step, size)) for i in range(size)])  6.16 us
    pallas_call x1, Pallas kernels, local(): pl.pallas_call(functools.partial(scores_kernel, groups), out_shape=[jax.S...  1.84 us
    pallas_call x1, Pallas kernels, local(): pl.pallas_call(round_kernel, out_shape=jax.ShapeDtypeStruct((per_group, c...  0.73 us
  transfers between devices with their start and end apart: 12, of which 10 were waited for; matrix products, arithmetic and copies ran while one was open for 0% of the time, Pallas kernels for 5%

profile of v1, /device:TPU:0, one launch (start us, length us, event | category | flops | bytes accessed | tf_op | source)
XLA Modules:
  0.0 35.0 jit_solution(2223174844008372329)
XLA Ops:
  0.6 1.8 %scores.1 = (bf16[256,256]{1,0:T(8,128)(2,1)S(1)}, bf16[128,256]{1,0:T(8,128)(2,1)S(1)}, s32[1,256]{1,0:T(1,128)S(1)}, bf16[256,2048]{1,0:T(8,128)(2,1)S(1)}) custom-call(bf16[512,512]{1,0:T(8,128)(2,1)} %table_ref.1, s32[1,256]{1,0:T(1,128)} %bitcast.6, bf16[256,512]{1,0:T(8,128)(2,1)} %basis_ref.1, s32[1,256]{1,0:T(1,128)} %bitcast.7, s32[4]{0:T(128)} %counts_ref.1, ...), custom_call_target="tpu_custom_call" | custom-call | tf_op jit(solution)/shard_map/scores/pallas_call | solution.py:236
  2.5 3.0 %collective-permute-start = (bf16[256,256]{1,0:T(8,128)(2,1)S(1)}, bf16[256,256]{1,0:T(8,128)(2,1)S(1)}, u32[]{:S(2)}, u32[]{:S(2)}) collective-permute-start(bf16[256,256]{1,0:T(8,128)(2,1)S(1)} %get-tuple-element.17.refs_0_), channel_id=1, source_target_pairs={{0,8},{1,17},{2,10},{3,19},{4,12},{5,21},{6,14},{7,23},{8,0},{9,25... | collective-permute-start | bytes 393224 | tf_op jit(solution)/shard_map/ppermute | solution.py:35
  5.5 1.5 %collective-permute-start.2 = (bf16[128,256]{1,0:T(8,128)(2,1)S(1)}, bf16[128,256]{1,0:T(8,128)(2,1)S(1)}, u32[]{:S(2)}, u32[]{:S(2)}) collective-permute-start(bf16[128,256]{1,0:T(8,128)(2,1)S(1)} %get-tuple-element.18), channel_id=1, source_target_pairs={{0,24},{8,16},{16,8},{24,0},{1,25},{9,17},{17,9},{25,1},{2,26},{10... | collective-permute-start | bytes 196616 | tf_op jit(solution)/shard_map/ppermute | solution.py:25
  7.0 2.2 %collective-permute-done.refs_1_ = bf16[256,256]{1,0:T(8,128)(2,1)S(1)} collective-permute-done((bf16[256,256]{1,0:T(8,128)(2,1)S(1)}, bf16[256,256]{1,0:T(8,128)(2,1)S(1)}, u32[]{:S(2)}, u32[]{:S(2)}) %collective-permute-start) | collective-permute-done | bytes 131104 | tf_op jit(solution)/shard_map/ppermute | solution.py:35
  9.2 0.0 collective-permute-start.1
  9.2 2.2 %collective-permute-done.2.refs_3_ = bf16[128,256]{1,0:T(8,128)(2,1)S(1)} collective-permute-done((bf16[128,256]{1,0:T(8,128)(2,1)S(1)}, bf16[128,256]{1,0:T(8,128)(2,1)S(1)}, u32[]{:S(2)}, u32[]{:S(2)}) %collective-permute-start.2) | collective-permute-done | bytes 65568 | tf_op jit(solution)/shard_map/ppermute | solution.py:25
  11.3 0.0 collective-permute-start.3
  11.3 0.1 picks.1.picks_ref
  11.5 1.1 %collective-permute-done.3.refs_4_ = bf16[128,256]{1,0:T(8,128)(2,1)S(1)} collective-permute-done((bf16[128,256]{1,0:T(8,128)(2,1)S(1)}, bf16[128,256]{1,0:T(8,128)(2,1)S(1)}, u32[]{:S(2)}, u32[]{:S(2)}) %collective-permute-start.3) | collective-permute-done | bytes 65568 | tf_op jit(solution)/shard_map/ppermute | solution.py:25
  12.6 0.0 collective-permute-done.1.refs_2_
  12.6 0.6 %first.1 = (bf16[64,1024]{1,0:T(8,128)(2,1)S(1)}, bf16[64,1024]{1,0:T(8,128)(2,1)S(1)}) custom-call(bf16[4,256,256]{2,1,0:T(8,128)(2,1)S(1)} %picks.1.picks_ref, bf16[256,2048]{1,0:T(8,128)(2,1)S(1)} %get-tuple-element.16.damage_ref, bf16[256,256]{1,0:T(8,128)(2,1)S(1)} %get-tuple-element.17.refs_0_, bf16[256,256]{1,0:T(8,128)(2,1)S(1)} %collective-permute-done.refs_1_, ...), custom_call_target="tpu_custom_call" | custom-call | flops 1048576 | bytes 1048576 | tf_op jit(solution)/shard_map/first/pallas_call | solution.py:283
  13.2 1.6 %collective-permute-start.5 = (bf16[64,1024]{1,0:T(8,128)(2,1)S(1)}, bf16[64,1024]{1,0:T(8,128)(2,1)S(1)}, u32[]{:S(2)}, u32[]{:S(2)}) collective-permute-start(bf16[64,1024]{1,0:T(8,128)(2,1)S(1)} %get-tuple-element.22), channel_id=1, source_target_pairs={{0,8},{1,17},{2,10},{3,19},{4,12},{5,21},{6,14},{7,23},{8,0},{9,25... | collective-permute-start | bytes 393224 | tf_op jit(solution)/shard_map/ppermute | solution.py:35
  14.8 0.5 %collective-permute-start.7 = (bf16[64,1024]{1,0:T(8,128)(2,1)S(1)}, bf16[64,1024]{1,0:T(8,128)(2,1)S(1)}, u32[]{:S(2)}, u32[]{:S(2)}) collective-permute-start(bf16[64,1024]{1,0:T(8,128)(2,1)S(1)} %get-tuple-element.24), channel_id=1, source_target_pairs={{0,8},{1,17},{2,10},{3,19},{4,12},{5,21},{6,14},{7,23},{8,0},{9,25... | collective-permute-start | bytes 393224 | tf_op jit(solution)/shard_map/ppermute | solution.py:35
  15.3 0.7 %other.1 = (bf16[64,2048]{1,0:T(8,128)(2,1)S(1)}, f32[64,1024]{1,0:T(8,128)S(1)}, f32[64,1024]{1,0:T(8,128)S(1)}, bf16[64,256]{1,0:T(8,128)(2,1)S(1)}) custom-call(bf16[4,256,256]{2,1,0:T(8,128)(2,1)S(1)} %picks.1.picks_ref, bf16[256,2048]{1,0:T(8,128)(2,1)S(1)} %get-tuple-element.16.damage_ref, bf16[256,256]{1,0:T(8,128)(2,1)S(1)} %get-tuple-element.17.refs_0_, ...), custom_call_target="tpu_custom_call" | custom-call | flops 1048576 | bytes 1048576 | tf_op jit(solution)/shard_map/other/pallas_call | solution.py:299
  16.0 1.6 %collective-permute-start.4 = (bf16[64,2048]{1,0:T(8,128)(2,1)S(1)}, bf16[64,2048]{1,0:T(8,128)(2,1)S(1)}, u32[]{:S(2)}, u32[]{:S(2)}) collective-permute-start(bf16[64,2048]{1,0:T(8,128)(2,1)S(1)} %get-tuple-element.20), channel_id=1, source_target_pairs={{0,8},{1,17},{2,10},{3,19},{4,12},{5,21},{6,14},{7,23},{8,0},{9,25... | collective-permute-start | bytes 786440 | tf_op jit(solution)/shard_map/ppermute | solution.py:35
  17.5 0.7 %collective-permute-done.5.two_ref = bf16[64,1024]{1,0:T(8,128)(2,1)S(1)} collective-permute-done((bf16[64,1024]{1,0:T(8,128)(2,1)S(1)}, bf16[64,1024]{1,0:T(8,128)(2,1)S(1)}, u32[]{:S(2)}, u32[]{:S(2)}) %collective-permute-start.5) | collective-permute-done | bytes 131104 | tf_op jit(solution)/shard_map/ppermute | solution.py:35
  18.3 0.9 %collective-permute-start.6 = (bf16[64,1024]{1,0:T(8,128)(2,1)S(1)}, bf16[64,1024]{1,0:T(8,128)(2,1)S(1)}, u32[]{:S(2)}, u32[]{:S(2)}) collective-permute-start(bf16[64,1024]{1,0:T(8,128)(2,1)S(1)} %add.33), channel_id=1, source_target_pairs={{0,16},{1,9},{2,18},{3,11},{4,20},{5,13},{6,22},{7,15},{8,24},{9,1... | collective-permute-start | bytes 393224 | tf_op jit(solution)/shard_map/ppermute | solution.py:35
  19.2 0.5 %collective-permute-done.7.two_ref = bf16[64,1024]{1,0:T(8,128)(2,1)S(1)} collective-permute-done((bf16[64,1024]{1,0:T(8,128)(2,1)S(1)}, bf16[64,1024]{1,0:T(8,128)(2,1)S(1)}, u32[]{:S(2)}, u32[]{:S(2)}) %collective-permute-start.7) | collective-permute-done | bytes 131104 | tf_op jit(solution)/shard_map/ppermute | solution.py:35
  19.8 0.8 %collective-permute-start.8 = (bf16[64,1024]{1,0:T(8,128)(2,1)S(1)}, bf16[64,1024]{1,0:T(8,128)(2,1)S(1)}, u32[]{:S(2)}, u32[]{:S(2)}) collective-permute-start(bf16[64,1024]{1,0:T(8,128)(2,1)S(1)} %add.34), channel_id=1, source_target_pairs={{0,16},{1,9},{2,18},{3,11},{4,20},{5,13},{6,22},{7,15},{8,24},{9,1... | collective-permute-start | bytes 393224 | tf_op jit(solution)/shard_map/ppermute | solution.py:35
  20.6 0.3 own.1.own_ref
  20.9 2.4 %collective-permute-done.6.refs_1_ = bf16[64,1024]{1,0:T(8,128)(2,1)S(1)} collective-permute-done((bf16[64,1024]{1,0:T(8,128)(2,1)S(1)}, bf16[64,1024]{1,0:T(8,128)(2,1)S(1)}, u32[]{:S(2)}, u32[]{:S(2)}) %collective-permute-start.6) | collective-permute-done | bytes 131104 | tf_op jit(solution)/shard_map/ppermute | solution.py:35
  23.3 1.5 %collective-permute-done.8.refs_2_ = bf16[64,1024]{1,0:T(8,128)(2,1)S(1)} collective-permute-done((bf16[64,1024]{1,0:T(8,128)(2,1)S(1)}, bf16[64,1024]{1,0:T(8,128)(2,1)S(1)}, u32[]{:S(2)}, u32[]{:S(2)}) %collective-permute-start.8) | collective-permute-done | bytes 131104 | tf_op jit(solution)/shard_map/ppermute | solution.py:35
  24.8 0.1 collective-permute-done.4.refs_0_
  24.8 0.2 values.1
  25.1 0.4 %collective-permute-start.9 = (f32[2,64]{1,0:T(2,128)S(1)}, f32[2,64]{1,0:T(2,128)S(1)}, u32[]{:S(2)}, u32[]{:S(2)}) collective-permute-start(f32[2,64]{1,0:T(2,128)S(1)} %get-tuple-element.26), channel_id=1, source_target_pairs={{0,1},{1,0},{2,3},{3,2},{4,5},{5,4},{6,7},{7,6},{8,9},{9,8},{10,11... | collective-permute-start | bytes 1544 | tf_op jit(solution)/shard_map/ppermute | solution.py:25
  25.4 0.8 %collective-permute-done.9 = f32[2,64]{1,0:T(2,128)S(1)} collective-permute-done((f32[2,64]{1,0:T(2,128)S(1)}, f32[2,64]{1,0:T(2,128)S(1)}, u32[]{:S(2)}, u32[]{:S(2)}) %collective-permute-start.9) | collective-permute-done | bytes 544 | tf_op jit(solution)/shard_map/ppermute | solution.py:25
  26.3 1.6 %collective-permute-start.10 = (f32[2,64]{1,0:T(2,128)S(1)}, f32[2,64]{1,0:T(2,128)S(1)}, u32[]{:S(2)}, u32[]{:S(2)}) collective-permute-start(f32[2,64]{1,0:T(2,128)S(1)} %pad_maximum_fusion), channel_id=1, source_target_pairs={{0,2},{1,3},{2,0},{3,1},{4,6},{5,7},{6,4},{7,5},{8,10},{9,11},{10,... | collective-permute-start | bytes 1544 | tf_op jit(solution)/shard_map/ppermute | solution.py:25
  27.9 2.0 %collective-permute-done.10 = f32[2,64]{1,0:T(2,128)S(1)} collective-permute-done((f32[2,64]{1,0:T(2,128)S(1)}, f32[2,64]{1,0:T(2,128)S(1)}, u32[]{:S(2)}, u32[]{:S(2)}) %collective-permute-start.10) | collective-permute-done | bytes 544 | tf_op jit(solution)/shard_map/ppermute | solution.py:25
  29.9 2.7 %collective-permute-start.11 = (f32[2,64]{1,0:T(2,128)S(1)}, f32[2,64]{1,0:T(2,128)S(1)}, u32[]{:S(2)}, u32[]{:S(2)}) collective-permute-start(f32[2,64]{1,0:T(2,128)S(1)} %pad_maximum_fusion.1), channel_id=1, source_target_pairs={{0,4},{1,5},{2,6},{3,7},{4,0},{5,1},{6,2},{7,3},{8,12},{9,13},{10,... | collective-permute-start | bytes 1544 | tf_op jit(solution)/shard_map/ppermute | solution.py:25
  32.6 0.7 %round.1 = bf16[64,2048]{1,0:T(8,128)(2,1)} custom-call(f32[64,2048]{1,0:T(8,128)S(1)} %get-tuple-element.25.values_ref), custom_call_target="tpu_custom_call" | custom-call | flops 1048576 | bytes 1048576 | tf_op jit(solution)/shard_map/round/pallas_call | solution.py:347
  33.3 1.1 %collective-permute-done.11 = f32[2,64]{1,0:T(2,128)S(1)} collective-permute-done((f32[2,64]{1,0:T(2,128)S(1)}, f32[2,64]{1,0:T(2,128)S(1)}, u32[]{:S(2)}, u32[]{:S(2)}) %collective-permute-start.11) | collective-permute-done | bytes 544 | tf_op jit(solution)/shard_map/ppermute | solution.py:25
  34.5 0.5 %sqrt_bitcast_fusion = (f32[64]{0:T(128)}, f32[64]{0:T(128)}) fusion(f32[1,64]{1,0:T(1,128)S(1)} %get-tuple-element.31, f32[2,64]{1,0:T(2,128)S(1)} %collective-permute-done.11, f32[1,64]{1,0:T(1,128)S(1)} %get-tuple-element.32), kind=kLoop, calls=%fused_computation.2 | loop fusion | flops 256 | bytes 1536 | tf_op jit(solution)/shard_map/sqrt | solution.py:358
  (6 shorter events, 0.1 us)
Async XLA Ops:
  2.5 6.7 %collective-permute-start = (bf16[256,256]{1,0:T(8,128)(2,1)S(1)}, bf16[256,256]{1,0:T(8,128)(2,1)S(1)}, u32[]{:S(2)}, u32[]{:S(2)}) collective-permute-start(bf16[256,256]{1,0:T(8,128)(2,1)S(1)} %get-tuple-element.17.refs_0_), channel_id=1, source_target_pairs={{0,8},{1,17},{2,10},{3,19},{4,12},{5,21},{6,14},{7,23},{8,0},{9,25... | collective-permute-start | bytes 393224 | tf_op jit(solution)/shard_map/ppermute | solution.py:35
  5.5 5.8 %collective-permute-start.2 = (bf16[128,256]{1,0:T(8,128)(2,1)S(1)}, bf16[128,256]{1,0:T(8,128)(2,1)S(1)}, u32[]{:S(2)}, u32[]{:S(2)}) collective-permute-start(bf16[128,256]{1,0:T(8,128)(2,1)S(1)} %get-tuple-element.18), channel_id=1, source_target_pairs={{0,24},{8,16},{16,8},{24,0},{1,25},{9,17},{17,9},{25,1},{2,26},{10... | collective-permute-start | bytes 196616 | tf_op jit(solution)/shard_map/ppermute | solution.py:25
  9.2 3.4 %collective-permute-start.1 = (bf16[256,256]{1,0:T(8,128)(2,1)S(1)}, bf16[256,256]{1,0:T(8,128)(2,1)S(1)}, u32[]{:S(2)}, u32[]{:S(2)}) collective-permute-start(bf16[256,256]{1,0:T(8,128)(2,1)S(1)} %collective-permute-done.refs_1_), channel_id=1, source_target_pairs={{0,1},{1,0},{2,3},{3,2},{4,5},{5,4},{6,7},{7,6},{8,9},{9,8},{10,11... | collective-permute-start | bytes 393224 | tf_op jit(solution)/shard_map/ppermute | solution.py:25
  11.3 1.3 %collective-permute-start.3 = (bf16[128,256]{1,0:T(8,128)(2,1)S(1)}, bf16[128,256]{1,0:T(8,128)(2,1)S(1)}, u32[]{:S(2)}, u32[]{:S(2)}) collective-permute-start(bf16[128,256]{1,0:T(8,128)(2,1)S(1)} %collective-permute-done.2.refs_3_), channel_id=1, source_target_pairs={{0,1},{1,0},{2,3},{3,2},{4,5},{5,4},{6,7},{7,6},{8,9},{9,8},{10,11... | collective-permute-start | bytes 196616 | tf_op jit(solution)/shard_map/ppermute | solution.py:25
  13.2 5.0 %collective-permute-start.5 = (bf16[64,1024]{1,0:T(8,128)(2,1)S(1)}, bf16[64,1024]{1,0:T(8,128)(2,1)S(1)}, u32[]{:S(2)}, u32[]{:S(2)}) collective-permute-start(bf16[64,1024]{1,0:T(8,128)(2,1)S(1)} %get-tuple-element.22), channel_id=1, source_target_pairs={{0,8},{1,17},{2,10},{3,19},{4,12},{5,21},{6,14},{7,23},{8,0},{9,25... | collective-permute-start | bytes 393224 | tf_op jit(solution)/shard_map/ppermute | solution.py:35
  14.8 5.0 %collective-permute-start.7 = (bf16[64,1024]{1,0:T(8,128)(2,1)S(1)}, bf16[64,1024]{1,0:T(8,128)(2,1)S(1)}, u32[]{:S(2)}, u32[]{:S(2)}) collective-permute-start(bf16[64,1024]{1,0:T(8,128)(2,1)S(1)} %get-tuple-element.24), channel_id=1, source_target_pairs={{0,8},{1,17},{2,10},{3,19},{4,12},{5,21},{6,14},{7,23},{8,0},{9,25... | collective-permute-start | bytes 393224 | tf_op jit(solution)/shard_map/ppermute | solution.py:35
  16.0 8.9 %collective-permute-start.4 = (bf16[64,2048]{1,0:T(8,128)(2,1)S(1)}, bf16[64,2048]{1,0:T(8,128)(2,1)S(1)}, u32[]{:S(2)}, u32[]{:S(2)}) collective-permute-start(bf16[64,2048]{1,0:T(8,128)(2,1)S(1)} %get-tuple-element.20), channel_id=1, source_target_pairs={{0,8},{1,17},{2,10},{3,19},{4,12},{5,21},{6,14},{7,23},{8,0},{9,25... | collective-permute-start | bytes 786440 | tf_op jit(solution)/shard_map/ppermute | solution.py:35
  18.3 5.0 %collective-permute-start.6 = (bf16[64,1024]{1,0:T(8,128)(2,1)S(1)}, bf16[64,1024]{1,0:T(8,128)(2,1)S(1)}, u32[]{:S(2)}, u32[]{:S(2)}) collective-permute-start(bf16[64,1024]{1,0:T(8,128)(2,1)S(1)} %add.33), channel_id=1, source_target_pairs={{0,16},{1,9},{2,18},{3,11},{4,20},{5,13},{6,22},{7,15},{8,24},{9,1... | collective-permute-start | bytes 393224 | tf_op jit(solution)/shard_map/ppermute | solution.py:35
  19.8 5.0 %collective-permute-start.8 = (bf16[64,1024]{1,0:T(8,128)(2,1)S(1)}, bf16[64,1024]{1,0:T(8,128)(2,1)S(1)}, u32[]{:S(2)}, u32[]{:S(2)}) collective-permute-start(bf16[64,1024]{1,0:T(8,128)(2,1)S(1)} %add.34), channel_id=1, source_target_pairs={{0,16},{1,9},{2,18},{3,11},{4,20},{5,13},{6,22},{7,15},{8,24},{9,1... | collective-permute-start | bytes 393224 | tf_op jit(solution)/shard_map/ppermute | solution.py:35
  25.1 1.2 %collective-permute-start.9 = (f32[2,64]{1,0:T(2,128)S(1)}, f32[2,64]{1,0:T(2,128)S(1)}, u32[]{:S(2)}, u32[]{:S(2)}) collective-permute-start(f32[2,64]{1,0:T(2,128)S(1)} %get-tuple-element.26), channel_id=1, source_target_pairs={{0,1},{1,0},{2,3},{3,2},{4,5},{5,4},{6,7},{7,6},{8,9},{9,8},{10,11... | collective-permute-start | bytes 1544 | tf_op jit(solution)/shard_map/ppermute | solution.py:25
  26.3 3.6 %collective-permute-start.10 = (f32[2,64]{1,0:T(2,128)S(1)}, f32[2,64]{1,0:T(2,128)S(1)}, u32[]{:S(2)}, u32[]{:S(2)}) collective-permute-start(f32[2,64]{1,0:T(2,128)S(1)} %pad_maximum_fusion), channel_id=1, source_target_pairs={{0,2},{1,3},{2,0},{3,1},{4,6},{5,7},{6,4},{7,5},{8,10},{9,11},{10,... | collective-permute-start | bytes 1544 | tf_op jit(solution)/shard_map/ppermute | solution.py:25
  29.9 4.5 %collective-permute-start.11 = (f32[2,64]{1,0:T(2,128)S(1)}, f32[2,64]{1,0:T(2,128)S(1)}, u32[]{:S(2)}, u32[]{:S(2)}) collective-permute-start(f32[2,64]{1,0:T(2,128)S(1)} %pad_maximum_fusion.1), channel_id=1, source_target_pairs={{0,4},{1,5},{2,6},{3,7},{4,0},{5,1},{6,2},{7,3},{8,12},{9,13},{10,... | collective-permute-start | bytes 1544 | tf_op jit(solution)/shard_map/ppermute | solution.py:25

commit v2 on v0

v2 whole, which is shorter than its diff:
```python
import functools

import jax
import jax.numpy as jnp
from jax import lax
from jax.experimental import pallas as pl
from jax.experimental.pallas import tpu as pltpu
from jax.sharding import PartitionSpec as P


FULL = pl.BlockSpec(memory_space=pltpu.VMEM)
FAR = pl.BlockSpec(memory_space=pltpu.HBM)


def mate(index, step, size):
    return index ^ step if size & (size - 1) == 0 else (index + step) % size


def origin(index, step, size):
    return index ^ step if size & (size - 1) == 0 else (index - step) % size


def swap(value, axis, step):
    size = lax.axis_size(axis)
    return lax.ppermute(value, axis, [(i, mate(i, step, size)) for i in range(size)])


def split_swap(value, steps):
    nodes = lax.axis_size("node")
    pairs = [
        (group * nodes + node, (group ^ steps[node % 2]) * nodes + node)
        for group in range(lax.axis_size("grp"))
        for node in range(nodes)
    ]
    return lax.ppermute(value, ("grp", "node"), pairs)


def scores_kernel(groups, table_ref, ids_ref, basis_ref, train_ref, counts_ref, damage_ref, *refs):
    (scores, named, damage), sends = refs[:3], refs[3:-7]
    table, ids, basis, train, counts, choice, sems = refs[-7:]
    pairs = (
        (ids_ref, ids),
        (table_ref, table),
        (basis_ref, basis),
        (counts_ref, counts),
        (train_ref, train),
        (damage_ref, damage),
    )
    copies = [pltpu.make_async_copy(src, dst, sems.at[k]) for k, (src, dst) in enumerate(pairs)]
    for copy in copies:
        copy.start()
    me = lax.axis_index("grp")
    samples = ids.shape[1]
    copies[0].wait()
    lane = lax.broadcasted_iota(jnp.int32, (samples, 128), 1)
    wanted = jnp.transpose(jnp.broadcast_to(ids[...].astype(jnp.float32), (128, samples)))
    for start in range(0, table.shape[0], 128):
        match = wanted == (lane + start).astype(jnp.float32)
        choice[:, start : start + 128] = match.astype(jnp.bfloat16)
    copies[1].wait()
    chosen = jnp.dot(choice[...], table[...], preferred_element_type=jnp.float32)
    copies[2].wait()
    found = lax.dot_general(
        chosen.astype(jnp.bfloat16),
        basis[...],
        (((1,), (1,)), ((), ())),
        preferred_element_type=jnp.float32,
    )
    copies[3].wait()
    total = lax.fori_loop(0, groups, lambda k, s: s + counts[k], jnp.int32(0)).astype(jnp.float32)
    scores[...] = (found / total).astype(jnp.bfloat16)
    if sends:
        odd = lax.axis_index("node") % 2
        near_head, near_tail, side_head, side_tail = sends
        per_group = near_head.shape[0]
        other = me ^ (1 + 2 * odd)
        near_head[...] = rows_of(scores, other ^ 3, per_group)
        for place, step in enumerate((1, 2, 0)):
            near_tail[place * per_group : (place + 1) * per_group, :] = rows_of(
                scores, other ^ step, per_group
            )
        small = per_group // 2
        side_head[...] = rows_of(scores, (me ^ 1) * 2 + odd, small)
        for place in range(3):
            piece = odd * 3 + place
            step = jnp.where(piece // 2 == 0, 1, jnp.where(piece // 2 == 1, 2, 0))
            side_tail[place * small : (place + 1) * small, :] = rows_of(
                scores, (me ^ 2 ^ step) * 2 + piece % 2, small
            )
    copies[4].wait()
    live = lax.broadcasted_iota(jnp.int32, named.shape, 1) < counts[me]
    named[...] = jnp.where(live, train[...], -1)
    copies[5].wait()


def rows_of(ref, block, rows):
    return ref[pl.ds(pl.multiple_of(block * rows, rows), rows), :]


def picks_kernel(groups, named_ref, out_ref):
    me = lax.axis_index("grp")
    row = lax.broadcasted_iota(jnp.int32, out_ref.shape[1:], 0)
    for step in range(groups):
        first = origin(me, step, groups) * out_ref.shape[1]
        out_ref[step] = jnp.where(row == named_ref[...] - first, 1.0, 0.0).astype(out_ref.dtype)


def join(half_ref, other_ref, joined):
    odd = lax.axis_index("node") % 2
    rows = half_ref.shape[0]
    joined[pl.ds(pl.multiple_of(odd * rows, rows), rows), :] = half_ref[...]
    joined[pl.ds(pl.multiple_of((1 - odd) * rows, rows), rows), :] = other_ref[...]


def project(weight, damage_ref, start, outs, tile):
    rows = weight.shape[0] // len(outs)
    for at in range(0, outs[0].shape[1], tile):
        part = jnp.dot(
            weight,
            damage_ref[:, start + at : start + at + tile],
            preferred_element_type=jnp.float32,
        )
        for k, out in enumerate(outs):
            out[:, at : at + tile] = part[k * rows : (k + 1) * rows, :].astype(out.dtype)


def first_kernel(tile, picks_ref, damage_ref, own, near, mated, half, other, weight, out, joined):
    odd = lax.axis_index("node") % 2
    join(half, other, joined)
    total = jnp.dot(
        rows_of(own, lax.axis_index("grp") ^ 3, near.shape[0]),
        picks_ref[0],
        preferred_element_type=jnp.float32,
    )
    for ref, step in ((near, 1 + 2 * odd), (mated, 3 - 2 * odd), (joined, 2)):
        total += jnp.dot(ref[...], picks_ref[step], preferred_element_type=jnp.float32)
    weight[...] = total.astype(weight.dtype)
    project(weight[...], damage_ref, 0, [out], tile)


def second_kernel(tile, weight_ref, damage_ref, out_ref):
    project(weight_ref[...], damage_ref, damage_ref.shape[1] - out_ref.shape[1], [out_ref], tile)


def other_kernel(tile, picks_ref, damage_ref, own, near, mated, half, other, *refs):
    sent, kept, later, weight, order, joined = refs
    odd = lax.axis_index("node") % 2
    me = lax.axis_index("grp")
    join(half, other, joined)
    rows = sent.shape[0]
    steps = (1 + odd, 2 - odd, 0)
    total = None
    for ref, step in ((own, 0), (near, 1 + 2 * odd), (mated, 3 - 2 * odd), (joined, 2)):
        for place, target in enumerate(steps):
            block = me ^ target if ref is own else (odd, 1 - odd, 2)[place]
            order[place * rows : (place + 1) * rows, :] = rows_of(ref, block, rows)
        part = jnp.dot(order[...], picks_ref[step], preferred_element_type=jnp.float32)
        total = part if total is None else total + part
    total = total.astype(jnp.bfloat16)
    weight[...] = total[2 * rows :, :]
    width = kept.shape[1]
    for start, keep in ((0, kept), (width, later)):
        for at in range(0, width, tile):
            part = jnp.dot(
                total[: 2 * rows, :],
                damage_ref[:, start + at : start + at + tile],
                preferred_element_type=jnp.float32,
            )
            sent[:, start + at : start + at + tile] = part[:rows, :].astype(sent.dtype)
            keep[:, at : at + tile] = part[rows:, :]


def direct_kernel(groups, tile, picks_ref, damage_ref, *refs):
    scores, outs, order = refs[:groups], refs[groups:-1], refs[-1]
    me = lax.axis_index("grp")
    rows = outs[0].shape[0]
    total = None
    for step in range(groups):
        for target in range(groups):
            order[target * rows : (target + 1) * rows, :] = rows_of(
                scores[step], mate(me, target, groups), rows
            )
        part = jnp.dot(order[...], picks_ref[step], preferred_element_type=jnp.float32)
        total = part if total is None else total + part
    project(total.astype(jnp.bfloat16), damage_ref, 0, outs, tile)


def own_kernel(tile, weight_ref, damage_ref, out_ref):
    project(weight_ref[...], damage_ref, 0, [out_ref], tile)


def add_kernel(one_ref, two_ref, out_ref):
    out_ref[...] = (one_ref[...] + two_ref[...].astype(jnp.float32)).astype(out_ref.dtype)


def values_kernel(own_ref, *refs):
    parts, (out_ref, stats_ref) = refs[:-2], refs[-2:]
    rows, cells = out_ref.shape
    square = peak = None
    width = min(part.shape[1] for part in parts)
    for start in range(0, cells, width):
        values = own_ref[:, start : start + width]
        place = 0
        for part in parts:
            if place <= start < place + part.shape[1]:
                values = values + part[:, start - place : start - place + width].astype(jnp.float32)
            place = (place + part.shape[1]) % cells
        out_ref[:, start : start + width] = values
        more = jnp.sum(values * values, axis=1, keepdims=True)
        high = jnp.max(values, axis=1, keepdims=True)
        square = more if square is None else square + more
        peak = high if peak is None else jnp.maximum(peak, high)
    stats_ref[0:1, :] = jnp.transpose(jnp.broadcast_to(square, (rows, 128)))[0:1, :]
    stats_ref[1:2, :] = jnp.transpose(jnp.broadcast_to(peak, (rows, 128)))[0:1, :]


def round_kernel(values_ref, out_ref):
    out_ref[...] = values_ref[...].astype(out_ref.dtype)


def combine(first, second):
    return jnp.stack([first[0] + second[0], jnp.maximum(first[1], second[1])])


def over_nodes(stats, nodes):
    if nodes & (nodes - 1):
        everything = lax.all_gather(stats, "node")
        return jnp.stack([jnp.sum(everything[:, 0], axis=0), jnp.max(everything[:, 1], axis=0)])
    step = 1
    while step < nodes:
        stats = combine(stats, swap(stats, "node", step))
        step *= 2
    return stats


def call(kernel, outs, ins, *args, scratch=(), limit=24):
    return pl.pallas_call(
        kernel,
        out_shape=[jax.ShapeDtypeStruct(shape, kind) for shape, kind in outs],
        in_specs=ins,
        out_specs=[FULL] * len(outs),
        scratch_shapes=list(scratch),
        compiler_params=pltpu.CompilerParams(vmem_limit_bytes=limit << 20),
        cost_estimate=pl.CostEstimate(flops=1 << 20, bytes_accessed=1 << 20, transcendentals=0),
    )(*args)


def local(damage, basis_table, train_ids, counts, new_table, new_ids):
    slots, cells = damage.shape
    groups = lax.axis_size("grp")
    nodes = lax.axis_size("node")
    samples = new_ids.shape[0]
    per_group = samples // groups
    rows = basis_table.shape[0]
    half, full = jnp.bfloat16, jnp.float32
    paired = is_paired(groups, nodes)
    operands = (new_table, new_ids.reshape(1, samples), basis_table, train_ids.reshape(1, slots), counts, damage)
    rest = samples - per_group
    sends = [(per_group, rows), (rest, rows), (per_group // 2, rows), (rest // 2, rows)]
    scores, named, damage, *sends = call(
        functools.partial(scores_kernel, groups),
        [((samples, rows), half), ((1, slots), jnp.int32), ((slots, cells), half)]
        + ([(shape, half) for shape in sends] if paired else []),
        [FAR] * 6,
        *[pltpu.with_memory_space_constraint(x, pltpu.HBM) for x in operands],
        scratch=[
            pltpu.VMEM(new_table.shape, half),
            pltpu.VMEM((1, samples), jnp.int32),
            pltpu.VMEM(basis_table.shape, half),
            pltpu.VMEM((1, slots), jnp.int32),
            pltpu.SMEM((groups,), jnp.int32),
            pltpu.VMEM((samples, new_table.shape[0]), half),
            pltpu.SemaphoreType.DMA((6,)),
        ],
        limit=32,
    )
    picks = call(
        functools.partial(picks_kernel, groups), [((groups, rows, slots), half)], [FULL], named
    )[0]
    part = ((per_group, cells), half)

    if paired:
        width = cells // 2
        tile = min(width, 512)
        piece = (per_group, width)
        near_head, near_tail, side_head, side_tail = sends
        side_head = swap(side_head, "grp", 2)
        near_head = split_swap(near_head, (1, 3))
        side_tail = swap(side_tail, "grp", 2)
        near_tail = split_swap(near_tail, (1, 3))
        heads = (near_head, swap(near_head, "node", 1), side_head, swap(side_head, "node", 1))
        tails = (near_tail, swap(near_tail, "node", 1), side_tail, swap(side_tail, "node", 1))
        weight, first = call(
            functools.partial(first_kernel, tile),
            [((per_group, slots), half), (piece, half)],
            [FULL] * 7,
            picks,
            damage,
            scores,
            *heads,
            scratch=[pltpu.VMEM((per_group, rows), half)],
        )
        second = call(
            functools.partial(second_kernel, tile), [(piece, half)], [FULL] * 2, weight, damage
        )[0]
        passed = [split_swap(x, (1, 2)) for x in (first, second)]
        sent, *kept, weight = call(
            functools.partial(other_kernel, tile),
            [part, (piece, full), (piece, full), ((per_group, slots), half)],
            [FULL] * 7,
            picks,
            damage,
            scores,
            *tails,
            scratch=[pltpu.VMEM((rest, rows), half)] * 2,
        )
        arrived = [split_swap(sent, (1, 2))]
        for k in range(2):
            both = call(add_kernel, [(piece, half)], [FULL] * 2, kept[k], passed[k])[0]
            arrived.append(split_swap(both, (2, 1)))
        own = call(
            functools.partial(own_kernel, tile), [((per_group, cells), full)], [FULL] * 2, weight, damage
        )[0]
    else:
        every = [scores] + [swap(scores, "grp", step) for step in range(1, groups)]
        own, *parts = call(
            functools.partial(direct_kernel, groups, min(cells, 512)),
            [((per_group, cells), full)] + [part] * (groups - 1),
            [FULL] * (2 + groups),
            picks,
            damage,
            *every,
            scratch=[pltpu.VMEM((samples, rows), half)],
            limit=32,
        )
        arrived = [swap(x, "grp", step) for step, x in enumerate(parts, 1)]

    values, stats = call(
        values_kernel,
        [((per_group, cells), full), ((2, per_group), full)],
        [FULL] * (1 + len(arrived)),
        own,
        *arrived,
    )
    surrogate = call(round_kernel, [part], [FULL], values)[0]
    squares, peak = over_nodes(stats, nodes)
    spread = jnp.sqrt(squares / (cells * nodes) + 1e-06)
    return (surrogate, peak, spread)


def is_paired(groups, nodes):
    return groups == 4 and nodes % 2 == 0


def solution(mesh):
    placed = (P("grp", "node"), P("grp", None), P("grp"), P(), P(), P())
    return jax.shard_map(
        local,
        mesh=mesh,
        in_specs=placed,
        out_specs=(P("grp", "node"), P("grp"), P("grp")),
        check_vma=False,
    )
```

time: 162 us -> 38.9 us (0.24)
  waiting for transfers between devices: 104 us -> 14.2 us
  blocking collectives: 25.9 us -> 0 us
  starting transfers between devices: 0.12 us -> 18.7 us
  between operations: 15.1 us -> 0.7 us
  matrix products: 5.73 us -> 0 us
  local copies, waits for them, and re-layouts: 5.73 us -> 0 us
  Pallas kernels: 0 us -> 4.68 us
  other arithmetic: 4.84 us -> 0.56 us
    reduce_scatter x1 -> x0, waiting for transfers between devices: 52.7 us -> none  [local(): lax.psum_scatter(product / sample_total, 'grp', scatter_dimension=0, tile...]
    all_gather x2 -> x0, waiting for transfers between devices: 50.8 us -> none  [the longest x1 33.3 us: local(): lax.all_gather(coef_share.astype(jnp.bfloat16), 'grp', axis=0, tiled=True)]
    ppermute x0 -> x16, starting transfers between devices: none -> 18.7 us  [the longest x7 10.8 us: split_swap(): return lax.ppermute(value, ('grp', 'node'), pairs)]
    unnamed x1 -> x0, blocking collectives: 16.2 us -> none
    ppermute x0 -> x16, waiting for transfers between devices: none -> 14.2 us  [the longest x7 7.1 us: split_swap(): return lax.ppermute(value, ('grp', 'node'), pairs)]
    all_gather x1 -> x0, blocking collectives: 9.7 us -> none  [local(): lax.all_gather(train_ids, 'grp', axis=0, tiled=True)]
    dot_general x2 -> x0, matrix products: 5.73 us -> none  [the longest x1 2.93 us: local(): jnp.dot(term_cols, lax.all_gather(coef_share.astype(jnp.bfloat16), 'grp',...]
    pallas_call x0 -> x10, Pallas kernels: none -> 4.68 us  [call(): pl.pallas_call(kernel, out_shape=[jax.ShapeDtypeStruct(shape, kind) for s...]
  transfers between devices with their start and end apart: 3 -> 16, of which waited for: 3 -> 10; matrix products, arithmetic and copies ran while one was open for 3% -> 0% of each run, Pallas kernels for 0% -> 7%
where the time goes in v2:
time: 38.9 us; the launch traced here: 38.8 us
  starting transfers between devices  18.7 us (48%)
  waiting for transfers between devices  14.2 us (37%)
  Pallas kernels  4.68 us (12%)
  between operations  0.7 us (2%)
  other arithmetic  0.56 us (1%)
    ppermute x7, starting transfers between devices, split_swap(): return lax.ppermute(value, ('grp', 'node'), pairs)  10.8 us
    ppermute x9, starting transfers between devices, swap(): lax.ppermute(value, axis, [(i, mate(i, step, size)) for i in range(size)])  7.83 us
    ppermute x7, waiting for transfers between devices, split_swap(): return lax.ppermute(value, ('grp', 'node'), pairs)  7.1 us
    ppermute x9, waiting for transfers between devices, swap(): lax.ppermute(value, axis, [(i, mate(i, step, size)) for i in range(size)])  7.06 us
    pallas_call x10, Pallas kernels, call(): pl.pallas_call(kernel, out_shape=[jax.ShapeDtypeStruct(shape, kind) for s...  4.68 us
  transfers between devices with their start and end apart: 16, of which 10 were waited for; matrix products, arithmetic and copies ran while one was open for 0% of the time, Pallas kernels for 7%

profile of v2, /device:TPU:0, one launch (start us, length us, event | category | flops | bytes accessed | tf_op | source)
XLA Modules:
  0.0 38.8 jit_solution(3332058832015107935)
XLA Ops:
  0.6 1.9 %shard_map.85 = (bf16[256,256]{1,0:T(8,128)(2,1)S(1)}, s32[1,256]{1,0:T(1,128)S(1)}, bf16[256,2048]{1,0:T(8,128)(2,1)S(1)}, bf16[64,256]{1,0:T(8,128)(2,1)S(1)},...) custom-call(bf16[512,512]{1,0:T(8,128)(2,1)} %table_ref.1, ...), custom_call_target="tpu_custom_call" | custom-call | flops 1048576 | bytes 1048576 | tf_op jit(solution)/shard_map/pallas_call | solution.py:237
  2.5 3.0 %collective-permute-start = (bf16[192,256]{1,0:T(8,128)(2,1)S(1)}, bf16[192,256]{1,0:T(8,128)(2,1)S(1)}, u32[]{:S(2)}, u32[]{:S(2)}) collective-permute-start(bf16[192,256]{1,0:T(8,128)(2,1)S(1)} %get-tuple-element.21), channel_id=1, source_target_pairs={{0,8},{1,25},{2,10},{3,27},{4,12},{5,29},{6,14},{7,31},{8,0},{9,17... | collective-permute-start | bytes 294920 | tf_op jit(solution)/shard_map/ppermute | solution.py:35
  5.6 1.5 %collective-permute-start.2 = (bf16[96,256]{1,0:T(8,128)(2,1)S(1)}, bf16[96,256]{1,0:T(8,128)(2,1)S(1)}, u32[]{:S(2)}, u32[]{:S(2)}) collective-permute-start(bf16[96,256]{1,0:T(8,128)(2,1)S(1)} %get-tuple-element.22), channel_id=1, source_target_pairs={{0,16},{8,24},{16,0},{24,8},{1,17},{9,25},{17,1},{25,9},{2,18},{10... | collective-permute-start | bytes 147464 | tf_op jit(solution)/shard_map/ppermute | solution.py:25
  7.1 1.8 %collective-permute-done.near = bf16[192,256]{1,0:T(8,128)(2,1)S(1)} collective-permute-done((bf16[192,256]{1,0:T(8,128)(2,1)S(1)}, bf16[192,256]{1,0:T(8,128)(2,1)S(1)}, u32[]{:S(2)}, u32[]{:S(2)}) %collective-permute-start) | collective-permute-done | bytes 98336 | tf_op jit(solution)/shard_map/ppermute | solution.py:35
  8.9 0.0 collective-permute-start.1
  8.9 2.2 %collective-permute-start.5 = (bf16[64,256]{1,0:T(8,128)(2,1)S(1)}, bf16[64,256]{1,0:T(8,128)(2,1)S(1)}, u32[]{:S(2)}, u32[]{:S(2)}) collective-permute-start(bf16[64,256]{1,0:T(8,128)(2,1)S(1)} %get-tuple-element.26), channel_id=1, source_target_pairs={{0,8},{1,25},{2,10},{3,27},{4,12},{5,29},{6,14},{7,31},{8,0},{9,17... | collective-permute-start | bytes 98312 | tf_op jit(solution)/shard_map/ppermute | solution.py:35
  11.1 0.0 collective-permute-done.2.half
  11.1 0.3 collective-permute-start.3
  11.4 1.4 %collective-permute-start.7 = (bf16[32,256]{1,0:T(8,128)(2,1)S(1)}, bf16[32,256]{1,0:T(8,128)(2,1)S(1)}, u32[]{:S(2)}, u32[]{:S(2)}) collective-permute-start(bf16[32,256]{1,0:T(8,128)(2,1)S(1)} %get-tuple-element.27), channel_id=1, source_target_pairs={{0,16},{8,24},{16,0},{24,8},{1,17},{9,25},{17,1},{25,9},{2,18},{10... | collective-permute-start | bytes 49160 | tf_op jit(solution)/shard_map/ppermute | solution.py:25
  12.7 0.4 %collective-permute-done.5.near = bf16[64,256]{1,0:T(8,128)(2,1)S(1)} collective-permute-done((bf16[64,256]{1,0:T(8,128)(2,1)S(1)}, bf16[64,256]{1,0:T(8,128)(2,1)S(1)}, u32[]{:S(2)}, u32[]{:S(2)}) %collective-permute-start.5) | collective-permute-done | bytes 32800 | tf_op jit(solution)/shard_map/ppermute | solution.py:35
  13.1 0.0 collective-permute-start.6
  13.1 2.0 %collective-permute-done.7.half = bf16[32,256]{1,0:T(8,128)(2,1)S(1)} collective-permute-done((bf16[32,256]{1,0:T(8,128)(2,1)S(1)}, bf16[32,256]{1,0:T(8,128)(2,1)S(1)}, u32[]{:S(2)}, u32[]{:S(2)}) %collective-permute-start.7) | collective-permute-done | bytes 16416 | tf_op jit(solution)/shard_map/ppermute | solution.py:25
  15.1 0.0 collective-permute-start.8
  15.1 0.1 shard_map.86.picks_ref
  15.2 1.1 %collective-permute-done.8.other = bf16[32,256]{1,0:T(8,128)(2,1)S(1)} collective-permute-done((bf16[32,256]{1,0:T(8,128)(2,1)S(1)}, bf16[32,256]{1,0:T(8,128)(2,1)S(1)}, u32[]{:S(2)}, u32[]{:S(2)}) %collective-permute-start.8) | collective-permute-done | bytes 16416 | tf_op jit(solution)/shard_map/ppermute | solution.py:25
  16.3 0.0 collective-permute-done.6.mated
  16.3 0.5 %shard_map.89 = (bf16[64,256]{1,0:T(8,128)(2,1)S(1)}, bf16[64,1024]{1,0:T(8,128)(2,1)S(1)}) custom-call(bf16[4,256,256]{2,1,0:T(8,128)(2,1)S(1)} %shard_map.86.picks_ref, bf16[256,2048]{1,0:T(8,128)(2,1)S(1)} %get-tuple-element.19.damage_ref, bf16[256,256]{1,0:T(8,128)(2,1)S(1)} %get-tuple-element.20.own, bf16[64,256]{1,0:T(8,128)(2,1)S(1)} %collective-permute-done.5.near, ...), custom_call_target="tpu_custom_call" | custom-call | flops 1048576 | bytes 1048576 | tf_op jit(solution)/shard_map/pallas_call | solution.py:237
  16.8 0.2 shard_map.91
  17.0 0.7 %collective-permute-start.11 = (bf16[64,1024]{1,0:T(8,128)(2,1)S(1)}, bf16[64,1024]{1,0:T(8,128)(2,1)S(1)}, u32[]{:S(2)}, u32[]{:S(2)}) collective-permute-start(bf16[64,1024]{1,0:T(8,128)(2,1)S(1)} %shard_map.91), channel_id=1, source_target_pairs={{0,8},{1,17},{2,10},{3,19},{4,12},{5,21},{6,14},{7,23},{8,0},{9,25... | collective-permute-start | bytes 393224 | tf_op jit(solution)/shard_map/ppermute | solution.py:35
  17.7 1.4 %collective-permute-start.9 = (bf16[64,1024]{1,0:T(8,128)(2,1)S(1)}, bf16[64,1024]{1,0:T(8,128)(2,1)S(1)}, u32[]{:S(2)}, u32[]{:S(2)}) collective-permute-start(bf16[64,1024]{1,0:T(8,128)(2,1)S(1)} %get-tuple-element.28), channel_id=1, source_target_pairs={{0,8},{1,17},{2,10},{3,19},{4,12},{5,21},{6,14},{7,23},{8,0},{9,25... | collective-permute-start | bytes 393224 | tf_op jit(solution)/shard_map/ppermute | solution.py:35
  19.1 0.0 collective-permute-done.3.other
  19.1 0.0 collective-permute-done.1.mated
  19.1 0.7 %shard_map.87 = (bf16[64,2048]{1,0:T(8,128)(2,1)S(1)}, f32[64,1024]{1,0:T(8,128)S(1)}, f32[64,1024]{1,0:T(8,128)S(1)}, bf16[64,256]{1,0:T(8,128)(2,1)S(1)}) custom-call(bf16[4,256,256]{2,1,0:T(8,128)(2,1)S(1)} %shard_map.86.picks_ref, bf16[256,2048]{1,0:T(8,128)(2,1)S(1)} %get-tuple-element.19.damage_ref, bf16[256,256]{1,0:T(8,128)(2,1)S(1)} %get-tuple-element.20.own, ...), custom_call_target="tpu_custom_call" | custom-call | flops 1048576 | bytes 1048576 | tf_op jit(solution)/shard_map/pallas_call | solution.py:237
  19.8 0.7 %collective-permute-start.4 = (bf16[64,2048]{1,0:T(8,128)(2,1)S(1)}, bf16[64,2048]{1,0:T(8,128)(2,1)S(1)}, u32[]{:S(2)}, u32[]{:S(2)}) collective-permute-start(bf16[64,2048]{1,0:T(8,128)(2,1)S(1)} %get-tuple-element.24), channel_id=1, source_target_pairs={{0,8},{1,17},{2,10},{3,19},{4,12},{5,21},{6,14},{7,23},{8,0},{9,25... | collective-permute-start | bytes 786440 | tf_op jit(solution)/shard_map/ppermute | solution.py:35
  20.5 1.6 %collective-permute-done.11.two_ref = bf16[64,1024]{1,0:T(8,128)(2,1)S(1)} collective-permute-done((bf16[64,1024]{1,0:T(8,128)(2,1)S(1)}, bf16[64,1024]{1,0:T(8,128)(2,1)S(1)}, u32[]{:S(2)}, u32[]{:S(2)}) %collective-permute-start.11) | collective-permute-done | bytes 131104 | tf_op jit(solution)/shard_map/ppermute | solution.py:35
  22.1 1.4 %collective-permute-start.12 = (bf16[64,1024]{1,0:T(8,128)(2,1)S(1)}, bf16[64,1024]{1,0:T(8,128)(2,1)S(1)}, u32[]{:S(2)}, u32[]{:S(2)}) collective-permute-start(bf16[64,1024]{1,0:T(8,128)(2,1)S(1)} %shard_map.92), channel_id=1, source_target_pairs={{0,16},{1,9},{2,18},{3,11},{4,20},{5,13},{6,22},{7,15},{8,24},{9,1... | collective-permute-start | bytes 393224 | tf_op jit(solution)/shard_map/ppermute | solution.py:35
  23.5 0.0 collective-permute-done.9.two_ref
  23.6 1.4 %collective-permute-start.10 = (bf16[64,1024]{1,0:T(8,128)(2,1)S(1)}, bf16[64,1024]{1,0:T(8,128)(2,1)S(1)}, u32[]{:S(2)}, u32[]{:S(2)}) collective-permute-start(bf16[64,1024]{1,0:T(8,128)(2,1)S(1)} %shard_map.90), channel_id=1, source_target_pairs={{0,16},{1,9},{2,18},{3,11},{4,20},{5,13},{6,22},{7,15},{8,24},{9,1... | collective-permute-start | bytes 393224 | tf_op jit(solution)/shard_map/ppermute | solution.py:35
  24.9 0.3 shard_map.88.own_ref
  25.2 1.9 %collective-permute-done.12.refs_2_ = bf16[64,1024]{1,0:T(8,128)(2,1)S(1)} collective-permute-done((bf16[64,1024]{1,0:T(8,128)(2,1)S(1)}, bf16[64,1024]{1,0:T(8,128)(2,1)S(1)}, u32[]{:S(2)}, u32[]{:S(2)}) %collective-permute-start.12) | collective-permute-done | bytes 131104 | tf_op jit(solution)/shard_map/ppermute | solution.py:35
  27.1 1.5 %collective-permute-done.10.refs_1_ = bf16[64,1024]{1,0:T(8,128)(2,1)S(1)} collective-permute-done((bf16[64,1024]{1,0:T(8,128)(2,1)S(1)}, bf16[64,1024]{1,0:T(8,128)(2,1)S(1)}, u32[]{:S(2)}, u32[]{:S(2)}) %collective-permute-start.10) | collective-permute-done | bytes 131104 | tf_op jit(solution)/shard_map/ppermute | solution.py:35
  28.6 0.0 collective-permute-done.4.refs_0_
  28.6 0.2 shard_map.93
  28.8 0.3 collective-permute-start.13
  29.2 0.9 %collective-permute-done.13 = f32[2,64]{1,0:T(2,128)S(1)} collective-permute-done((f32[2,64]{1,0:T(2,128)S(1)}, f32[2,64]{1,0:T(2,128)S(1)}, u32[]{:S(2)}, u32[]{:S(2)}) %collective-permute-start.13) | collective-permute-done | bytes 544 | tf_op jit(solution)/shard_map/ppermute | solution.py:25
  30.0 1.6 %collective-permute-start.14 = (f32[2,64]{1,0:T(2,128)S(1)}, f32[2,64]{1,0:T(2,128)S(1)}, u32[]{:S(2)}, u32[]{:S(2)}) collective-permute-start(f32[2,64]{1,0:T(2,128)S(1)} %pad_maximum_fusion), channel_id=1, source_target_pairs={{0,2},{1,3},{2,0},{3,1},{4,6},{5,7},{6,4},{7,5},{8,10},{9,11},{10,... | collective-permute-start | bytes 1544 | tf_op jit(solution)/shard_map/ppermute | solution.py:25
  31.7 2.0 %collective-permute-done.14 = f32[2,64]{1,0:T(2,128)S(1)} collective-permute-done((f32[2,64]{1,0:T(2,128)S(1)}, f32[2,64]{1,0:T(2,128)S(1)}, u32[]{:S(2)}, u32[]{:S(2)}) %collective-permute-start.14) | collective-permute-done | bytes 544 | tf_op jit(solution)/shard_map/ppermute | solution.py:25
  33.7 2.7 %collective-permute-start.15 = (f32[2,64]{1,0:T(2,128)S(1)}, f32[2,64]{1,0:T(2,128)S(1)}, u32[]{:S(2)}, u32[]{:S(2)}) collective-permute-start(f32[2,64]{1,0:T(2,128)S(1)} %pad_maximum_fusion.1), channel_id=1, source_target_pairs={{0,4},{1,5},{2,6},{3,7},{4,0},{5,1},{6,2},{7,3},{8,12},{9,13},{10,... | collective-permute-start | bytes 1544 | tf_op jit(solution)/shard_map/ppermute | solution.py:25
  36.3 0.7 %shard_map.94 = bf16[64,2048]{1,0:T(8,128)(2,1)} custom-call(f32[64,2048]{1,0:T(8,128)S(1)} %get-tuple-element.31.values_ref), custom_call_target="tpu_custom_call" | custom-call | flops 1048576 | bytes 1048576 | tf_op jit(solution)/shard_map/pallas_call | solution.py:237
  37.1 1.2 %collective-permute-done.15 = f32[2,64]{1,0:T(2,128)S(1)} collective-permute-done((f32[2,64]{1,0:T(2,128)S(1)}, f32[2,64]{1,0:T(2,128)S(1)}, u32[]{:S(2)}, u32[]{:S(2)}) %collective-permute-start.15) | collective-permute-done | bytes 544 | tf_op jit(solution)/shard_map/ppermute | solution.py:25
  38.2 0.5 %sqrt_bitcast_fusion = (f32[64]{0:T(128)}, f32[64]{0:T(128)}) fusion(f32[1,64]{1,0:T(1,128)S(1)} %get-tuple-element.37, f32[2,64]{1,0:T(2,128)S(1)} %collective-permute-done.15, f32[1,64]{1,0:T(1,128)S(1)} %get-tuple-element.38), kind=kLoop, calls=%fused_computation.2 | loop fusion | flops 256 | bytes 1536 | tf_op jit(solution)/shard_map/sqrt | solution.py:347
  (6 shorter events, 0.1 us)
Async XLA Ops:
  2.5 6.3 %collective-permute-start = (bf16[192,256]{1,0:T(8,128)(2,1)S(1)}, bf16[192,256]{1,0:T(8,128)(2,1)S(1)}, u32[]{:S(2)}, u32[]{:S(2)}) collective-permute-start(bf16[192,256]{1,0:T(8,128)(2,1)S(1)} %get-tuple-element.21), channel_id=1, source_target_pairs={{0,8},{1,25},{2,10},{3,27},{4,12},{5,29},{6,14},{7,31},{8,0},{9,17... | collective-permute-start | bytes 294920 | tf_op jit(solution)/shard_map/ppermute | solution.py:35
  5.6 5.5 %collective-permute-start.2 = (bf16[96,256]{1,0:T(8,128)(2,1)S(1)}, bf16[96,256]{1,0:T(8,128)(2,1)S(1)}, u32[]{:S(2)}, u32[]{:S(2)}) collective-permute-start(bf16[96,256]{1,0:T(8,128)(2,1)S(1)} %get-tuple-element.22), channel_id=1, source_target_pairs={{0,16},{8,24},{16,0},{24,8},{1,17},{9,25},{17,1},{25,9},{2,18},{10... | collective-permute-start | bytes 147464 | tf_op jit(solution)/shard_map/ppermute | solution.py:25
  8.9 10.3 %collective-permute-start.1 = (bf16[192,256]{1,0:T(8,128)(2,1)S(1)}, bf16[192,256]{1,0:T(8,128)(2,1)S(1)}, u32[]{:S(2)}, u32[]{:S(2)}) collective-permute-start(bf16[192,256]{1,0:T(8,128)(2,1)S(1)} %collective-permute-done.near), channel_id=1, source_target_pairs={{0,1},{1,0},{2,3},{3,2},{4,5},{5,4},{6,7},{7,6},{8,9},{9,8},{10,11... | collective-permute-start | bytes 294920 | tf_op jit(solution)/shard_map/ppermute | solution.py:25
  8.9 4.3 %collective-permute-start.5 = (bf16[64,256]{1,0:T(8,128)(2,1)S(1)}, bf16[64,256]{1,0:T(8,128)(2,1)S(1)}, u32[]{:S(2)}, u32[]{:S(2)}) collective-permute-start(bf16[64,256]{1,0:T(8,128)(2,1)S(1)} %get-tuple-element.26), channel_id=1, source_target_pairs={{0,8},{1,25},{2,10},{3,27},{4,12},{5,29},{6,14},{7,31},{8,0},{9,17... | collective-permute-start | bytes 98312 | tf_op jit(solution)/shard_map/ppermute | solution.py:35
  11.1 8.1 %collective-permute-start.3 = (bf16[96,256]{1,0:T(8,128)(2,1)S(1)}, bf16[96,256]{1,0:T(8,128)(2,1)S(1)}, u32[]{:S(2)}, u32[]{:S(2)}) collective-permute-start(bf16[96,256]{1,0:T(8,128)(2,1)S(1)} %collective-permute-done.2.half), channel_id=1, source_target_pairs={{0,1},{1,0},{2,3},{3,2},{4,5},{5,4},{6,7},{7,6},{8,9},{9,8},{10,11... | collective-permute-start | bytes 147464 | tf_op jit(solution)/shard_map/ppermute | solution.py:25
  11.4 3.7 %collective-permute-start.7 = (bf16[32,256]{1,0:T(8,128)(2,1)S(1)}, bf16[32,256]{1,0:T(8,128)(2,1)S(1)}, u32[]{:S(2)}, u32[]{:S(2)}) collective-permute-start(bf16[32,256]{1,0:T(8,128)(2,1)S(1)} %get-tuple-element.27), channel_id=1, source_target_pairs={{0,16},{8,24},{16,0},{24,8},{1,17},{9,25},{17,1},{25,9},{2,18},{10... | collective-permute-start | bytes 49160 | tf_op jit(solution)/shard_map/ppermute | solution.py:25
  13.1 3.1 %collective-permute-start.6 = (bf16[64,256]{1,0:T(8,128)(2,1)S(1)}, bf16[64,256]{1,0:T(8,128)(2,1)S(1)}, u32[]{:S(2)}, u32[]{:S(2)}) collective-permute-start(bf16[64,256]{1,0:T(8,128)(2,1)S(1)} %collective-permute-done.5.near), channel_id=1, source_target_pairs={{0,1},{1,0},{2,3},{3,2},{4,5},{5,4},{6,7},{7,6},{8,9},{9,8},{10,11... | collective-permute-start | bytes 98312 | tf_op jit(solution)/shard_map/ppermute | solution.py:25
  15.1 1.2 %collective-permute-start.8 = (bf16[32,256]{1,0:T(8,128)(2,1)S(1)}, bf16[32,256]{1,0:T(8,128)(2,1)S(1)}, u32[]{:S(2)}, u32[]{:S(2)}) collective-permute-start(bf16[32,256]{1,0:T(8,128)(2,1)S(1)} %collective-permute-done.7.half), channel_id=1, source_target_pairs={{0,1},{1,0},{2,3},{3,2},{4,5},{5,4},{6,7},{7,6},{8,9},{9,8},{10,11... | collective-permute-start | bytes 49160 | tf_op jit(solution)/shard_map/ppermute | solution.py:25
  17.0 5.0 %collective-permute-start.11 = (bf16[64,1024]{1,0:T(8,128)(2,1)S(1)}, bf16[64,1024]{1,0:T(8,128)(2,1)S(1)}, u32[]{:S(2)}, u32[]{:S(2)}) collective-permute-start(bf16[64,1024]{1,0:T(8,128)(2,1)S(1)} %shard_map.91), channel_id=1, source_target_pairs={{0,8},{1,17},{2,10},{3,19},{4,12},{5,21},{6,14},{7,23},{8,0},{9,25... | collective-permute-start | bytes 393224 | tf_op jit(solution)/shard_map/ppermute | solution.py:35
  17.7 5.8 %collective-permute-start.9 = (bf16[64,1024]{1,0:T(8,128)(2,1)S(1)}, bf16[64,1024]{1,0:T(8,128)(2,1)S(1)}, u32[]{:S(2)}, u32[]{:S(2)}) collective-permute-start(bf16[64,1024]{1,0:T(8,128)(2,1)S(1)} %get-tuple-element.28), channel_id=1, source_target_pairs={{0,8},{1,17},{2,10},{3,19},{4,12},{5,21},{6,14},{7,23},{8,0},{9,25... | collective-permute-start | bytes 393224 | tf_op jit(solution)/shard_map/ppermute | solution.py:35
  19.8 8.8 %collective-permute-start.4 = (bf16[64,2048]{1,0:T(8,128)(2,1)S(1)}, bf16[64,2048]{1,0:T(8,128)(2,1)S(1)}, u32[]{:S(2)}, u32[]{:S(2)}) collective-permute-start(bf16[64,2048]{1,0:T(8,128)(2,1)S(1)} %get-tuple-element.24), channel_id=1, source_target_pairs={{0,8},{1,17},{2,10},{3,19},{4,12},{5,21},{6,14},{7,23},{8,0},{9,25... | collective-permute-start | bytes 786440 | tf_op jit(solution)/shard_map/ppermute | solution.py:35
  22.1 5.0 %collective-permute-start.12 = (bf16[64,1024]{1,0:T(8,128)(2,1)S(1)}, bf16[64,1024]{1,0:T(8,128)(2,1)S(1)}, u32[]{:S(2)}, u32[]{:S(2)}) collective-permute-start(bf16[64,1024]{1,0:T(8,128)(2,1)S(1)} %shard_map.92), channel_id=1, source_target_pairs={{0,16},{1,9},{2,18},{3,11},{4,20},{5,13},{6,22},{7,15},{8,24},{9,1... | collective-permute-start | bytes 393224 | tf_op jit(solution)/shard_map/ppermute | solution.py:35
  23.6 5.0 %collective-permute-start.10 = (bf16[64,1024]{1,0:T(8,128)(2,1)S(1)}, bf16[64,1024]{1,0:T(8,128)(2,1)S(1)}, u32[]{:S(2)}, u32[]{:S(2)}) collective-permute-start(bf16[64,1024]{1,0:T(8,128)(2,1)S(1)} %shard_map.90), channel_id=1, source_target_pairs={{0,16},{1,9},{2,18},{3,11},{4,20},{5,13},{6,22},{7,15},{8,24},{9,1... | collective-permute-start | bytes 393224 | tf_op jit(solution)/shard_map/ppermute | solution.py:35
  28.8 1.2 %collective-permute-start.13 = (f32[2,64]{1,0:T(2,128)S(1)}, f32[2,64]{1,0:T(2,128)S(1)}, u32[]{:S(2)}, u32[]{:S(2)}) collective-permute-start(f32[2,64]{1,0:T(2,128)S(1)} %get-tuple-element.32), channel_id=1, source_target_pairs={{0,1},{1,0},{2,3},{3,2},{4,5},{5,4},{6,7},{7,6},{8,9},{9,8},{10,11... | collective-permute-start | bytes 1544 | tf_op jit(solution)/shard_map/ppermute | solution.py:25
  30.0 3.6 %collective-permute-start.14 = (f32[2,64]{1,0:T(2,128)S(1)}, f32[2,64]{1,0:T(2,128)S(1)}, u32[]{:S(2)}, u32[]{:S(2)}) collective-permute-start(f32[2,64]{1,0:T(2,128)S(1)} %pad_maximum_fusion), channel_id=1, source_target_pairs={{0,2},{1,3},{2,0},{3,1},{4,6},{5,7},{6,4},{7,5},{8,10},{9,11},{10,... | collective-permute-start | bytes 1544 | tf_op jit(solution)/shard_map/ppermute | solution.py:25
  33.7 4.5 %collective-permute-start.15 = (f32[2,64]{1,0:T(2,128)S(1)}, f32[2,64]{1,0:T(2,128)S(1)}, u32[]{:S(2)}, u32[]{:S(2)}) collective-permute-start(f32[2,64]{1,0:T(2,128)S(1)} %pad_maximum_fusion.1), channel_id=1, source_target_pairs={{0,4},{1,5},{2,6},{3,7},{4,0},{5,1},{6,2},{7,3},{8,12},{9,13},{10,... | collective-permute-start | bytes 1544 | tf_op jit(solution)/shard_map/ppermute | solution.py:25

commit v3 on v2

--- a/solution.py
+++ b/solution.py
@@ -1,4 +1,5 @@
 import functools
+import math
 
 import jax
 import jax.numpy as jnp
@@ -33,6 +34,11 @@
         for node in range(nodes)
     ]
     return lax.ppermute(value, ("grp", "node"), pairs)
+
+
+def node_swap(value, steps):
+    pairs = [(node, node ^ steps[node % 2]) for node in range(lax.axis_size("node"))]
+    return lax.ppermute(value, "node", pairs)
 
 
 def scores_kernel(groups, table_ref, ids_ref, basis_ref, train_ref, counts_ref, damage_ref, *refs):
@@ -68,7 +74,7 @@
     )
     copies[3].wait()
     total = lax.fori_loop(0, groups, lambda k, s: s + counts[k], jnp.int32(0)).astype(jnp.float32)
-    scores[...] = (found / total).astype(jnp.bfloat16)
+    scores[...] = (found * (1.0 / total)).astype(jnp.bfloat16)
     if sends:
         odd = lax.axis_index("node") % 2
         near_head, near_tail, side_head, side_tail = sends
@@ -158,9 +164,8 @@
         total = part if total is None else total + part
     total = total.astype(jnp.bfloat16)
     weight[...] = total[2 * rows :, :]
-    width = kept.shape[1]
-    for start, keep in ((0, kept), (width, later)):
-        for at in range(0, width, tile):
+    for start, keep in ((0, kept), (kept.shape[1], later)):
+        for at in range(0, keep.shape[1], tile):
             part = jnp.dot(
                 total[: 2 * rows, :],
                 damage_ref[:, start + at : start + at + tile],
@@ -197,7 +202,7 @@
     parts, (out_ref, stats_ref) = refs[:-2], refs[-2:]
     rows, cells = out_ref.shape
     square = peak = None
-    width = min(part.shape[1] for part in parts)
+    width = math.gcd(512, *[part.shape[1] for part in parts])
     for start in range(0, cells, width):
         values = own_ref[:, start : start + width]
         place = 0
@@ -226,6 +231,11 @@
     if nodes & (nodes - 1):
         everything = lax.all_gather(stats, "node")
         return jnp.stack([jnp.sum(everything[:, 0], axis=0), jnp.max(everything[:, 1], axis=0)])
+    if nodes == 8:
+        pair = combine(stats, node_swap(stats, (1, 1)))
+        across = node_swap(pair, (4, 6))
+        beside = node_swap(pair, (2, 2))
+        return combine(combine(pair, beside), combine(across, node_swap(across, (1, 1))))
     step = 1
     while step < nodes:
         stats = combine(stats, swap(stats, "node", step))
@@ -280,9 +290,9 @@
     part = ((per_group, cells), half)
 
     if paired:
-        width = cells // 2
-        tile = min(width, 512)
-        piece = (per_group, width)
+        widths = split_columns(cells)
+        tile = math.gcd(512, *widths)
+        pieces = [(per_group, width) for width in widths]
         near_head, near_tail, side_head, side_tail = sends
         side_head = swap(side_head, "grp", 2)
         near_head = split_swap(near_head, (1, 3))
@@ -292,7 +302,7 @@
         tails = (near_tail, swap(near_tail, "node", 1), side_tail, swap(side_tail, "node", 1))
         weight, first = call(
             functools.partial(first_kernel, tile),
-            [((per_group, slots), half), (piece, half)],
+            [((per_group, slots), half), (pieces[0], half)],
             [FULL] * 7,
             picks,
             damage,
@@ -301,12 +311,12 @@
             scratch=[pltpu.VMEM((per_group, rows), half)],
         )
         second = call(
-            functools.partial(second_kernel, tile), [(piece, half)], [FULL] * 2, weight, damage
+            functools.partial(second_kernel, tile), [(pieces[1], half)], [FULL] * 2, weight, damage
         )[0]
         passed = [split_swap(x, (1, 2)) for x in (first, second)]
         sent, *kept, weight = call(
             functools.partial(other_kernel, tile),
-            [part, (piece, full), (piece, full), ((per_group, slots), half)],
+            [part, (pieces[0], full), (pieces[1], full), ((per_group, slots), half)],
             [FULL] * 7,
             picks,
             damage,
@@ -316,7 +326,7 @@
         )
         arrived = [split_swap(sent, (1, 2))]
         for k in range(2):
-            both = call(add_kernel, [(piece, half)], [FULL] * 2, kept[k], passed[k])[0]
+            both = call(add_kernel, [(pieces[k], half)], [FULL] * 2, kept[k], passed[k])[0]
             arrived.append(split_swap(both, (2, 1)))
         own = call(
             functools.partial(own_kernel, tile), [((per_group, cells), full)], [FULL] * 2, weight, damage
@@ -348,6 +358,11 @@
     return (surrogate, peak, spread)
 
 
+def split_columns(cells):
+    late = cells // 4
+    return cells - late, late
+
+
 def is_paired(groups, nodes):
     return groups == 4 and nodes % 2 == 0
 

time: 38.9 us -> 41.9 us (1.077)
  waiting for transfers between devices: 14.2 us -> 16.9 us
    ppermute x0 -> x4, starting transfers between devices: none -> 4.94 us  [node_swap(): return lax.ppermute(value, 'node', pairs)]
    ppermute x9 -> x6, starting transfers between devices: 7.83 us -> 3.51 us  [swap(): lax.ppermute(value, axis, [(i, mate(i, step, size)) for i in range(size)])]
    ppermute x0 -> x4, waiting for transfers between devices: none -> 2.14 us  [node_swap(): return lax.ppermute(value, 'node', pairs)]
    ppermute x7, waiting for transfers between devices: 7.1 us -> 7.99 us  [split_swap(): return lax.ppermute(value, ('grp', 'node'), pairs)]
    ppermute x7, starting transfers between devices: 10.8 us -> 10.4 us  [split_swap(): return lax.ppermute(value, ('grp', 'node'), pairs)]
    ppermute x9 -> x6, waiting for transfers between devices: 7.06 us -> 6.74 us  [swap(): lax.ppermute(value, axis, [(i, mate(i, step, size)) for i in range(size)])]
  transfers between devices with their start and end apart: 16 -> 17, of which waited for: 10 -> 8; matrix products, arithmetic and copies ran while one was open for 0% -> 0% of each run, Pallas kernels for 7% -> 6%
where the time goes in v3:
time: 41.9 us; the launch traced here: 41.7 us
  starting transfers between devices  18.8 us (45%)
  waiting for transfers between devices  16.9 us (40%)
  Pallas kernels  4.73 us (11%)
  between operations  0.71 us (2%)
  other arithmetic  0.54 us (1%)
    ppermute x7, starting transfers between devices, split_swap(): return lax.ppermute(value, ('grp', 'node'), pairs)  10.4 us
    ppermute x7, waiting for transfers between devices, split_swap(): return lax.ppermute(value, ('grp', 'node'), pairs)  7.99 us
    ppermute x6, waiting for transfers between devices, swap(): lax.ppermute(value, axis, [(i, mate(i, step, size)) for i in range(size)])  6.74 us
    ppermute x4, starting transfers between devices, node_swap(): return lax.ppermute(value, 'node', pairs)  4.94 us
    pallas_call x10, Pallas kernels, call(): pl.pallas_call(kernel, out_shape=[jax.ShapeDtypeStruct(shape, kind) for s...  4.73 us
    ppermute x6, starting transfers between devices, swap(): lax.ppermute(value, axis, [(i, mate(i, step, size)) for i in range(size)])  3.51 us
    ppermute x4, waiting for transfers between devices, node_swap(): return lax.ppermute(value, 'node', pairs)  2.14 us
  transfers between devices with their start and end apart: 17, of which 8 were waited for; matrix products, arithmetic and copies ran while one was open for 0% of the time, Pallas kernels for 6%

profile of v3, /device:TPU:0, one launch (start us, length us, event | category | flops | bytes accessed | tf_op | source)
XLA Modules:
  0.0 41.7 jit_solution(9925328160486694478)
XLA Ops:
  0.6 1.9 %shard_map.85 = (bf16[256,256]{1,0:T(8,128)(2,1)S(1)}, s32[1,256]{1,0:T(1,128)S(1)}, bf16[256,2048]{1,0:T(8,128)(2,1)S(1)}, bf16[64,256]{1,0:T(8,128)(2,1)S(1)},...) custom-call(bf16[512,512]{1,0:T(8,128)(2,1)} %table_ref.1, ...), custom_call_target="tpu_custom_call" | custom-call | flops 1048576 | bytes 1048576 | tf_op jit(solution)/shard_map/pallas_call | solution.py:247
  2.6 3.0 %collective-permute-start.5 = (bf16[64,256]{1,0:T(8,128)(2,1)S(1)}, bf16[64,256]{1,0:T(8,128)(2,1)S(1)}, u32[]{:S(2)}, u32[]{:S(2)}) collective-permute-start(bf16[64,256]{1,0:T(8,128)(2,1)S(1)} %get-tuple-element.26), channel_id=1, source_target_pairs={{0,8},{1,25},{2,10},{3,27},{4,12},{5,29},{6,14},{7,31},{8,0},{9,17... | collective-permute-start | bytes 98312 | tf_op jit(solution)/shard_map/ppermute | solution.py:36
  5.6 0.1 collective-permute-start
  5.7 2.0 %collective-permute-start.7 = (bf16[32,256]{1,0:T(8,128)(2,1)S(1)}, bf16[32,256]{1,0:T(8,128)(2,1)S(1)}, u32[]{:S(2)}, u32[]{:S(2)}) collective-permute-start(bf16[32,256]{1,0:T(8,128)(2,1)S(1)} %get-tuple-element.27), channel_id=1, source_target_pairs={{0,16},{8,24},{16,0},{24,8},{1,17},{9,25},{17,1},{25,9},{2,18},{10... | collective-permute-start | bytes 49160 | tf_op jit(solution)/shard_map/ppermute | solution.py:26
  7.6 0.0 collective-permute-done.5.near
  7.6 0.0 collective-permute-start.6
  7.7 1.8 %collective-permute-done.7.half = bf16[32,256]{1,0:T(8,128)(2,1)S(1)} collective-permute-done((bf16[32,256]{1,0:T(8,128)(2,1)S(1)}, bf16[32,256]{1,0:T(8,128)(2,1)S(1)}, u32[]{:S(2)}, u32[]{:S(2)}) %collective-permute-start.7) | collective-permute-done | bytes 16416 | tf_op jit(solution)/shard_map/ppermute | solution.py:26
  9.4 0.0 collective-permute-start.8
  9.4 0.1 shard_map.86.picks_ref
  9.5 1.1 %collective-permute-done.8.other = bf16[32,256]{1,0:T(8,128)(2,1)S(1)} collective-permute-done((bf16[32,256]{1,0:T(8,128)(2,1)S(1)}, bf16[32,256]{1,0:T(8,128)(2,1)S(1)}, u32[]{:S(2)}, u32[]{:S(2)}) %collective-permute-start.8) | collective-permute-done | bytes 16416 | tf_op jit(solution)/shard_map/ppermute | solution.py:26
  10.6 0.0 collective-permute-done.6.mated
  10.6 0.6 %shard_map.89 = (bf16[64,256]{1,0:T(8,128)(2,1)S(1)}, bf16[64,1536]{1,0:T(8,128)(2,1)S(1)}) custom-call(bf16[4,256,256]{2,1,0:T(8,128)(2,1)S(1)} %shard_map.86.picks_ref, bf16[256,2048]{1,0:T(8,128)(2,1)S(1)} %get-tuple-element.19.damage_ref, bf16[256,256]{1,0:T(8,128)(2,1)S(1)} %get-tuple-element.20.own, bf16[64,256]{1,0:T(8,128)(2,1)S(1)} %collective-permute-done.5.near, ...), custom_call_target="tpu_custom_call" | custom-call | flops 1048576 | bytes 1048576 | tf_op jit(solution)/shard_map/pallas_call | solution.py:247
  11.2 2.2 %collective-permute-start.9 = (bf16[64,1536]{1,0:T(8,128)(2,1)S(1)}, bf16[64,1536]{1,0:T(8,128)(2,1)S(1)}, u32[]{:S(2)}, u32[]{:S(2)}) collective-permute-start(bf16[64,1536]{1,0:T(8,128)(2,1)S(1)} %get-tuple-element.28), channel_id=1, source_target_pairs={{0,8},{1,17},{2,10},{3,19},{4,12},{5,21},{6,14},{7,23},{8,0},{9,25... | collective-permute-start | bytes 589832 | tf_op jit(solution)/shard_map/ppermute | solution.py:36
  13.3 1.5 %collective-permute-start.2 = (bf16[96,256]{1,0:T(8,128)(2,1)S(1)}, bf16[96,256]{1,0:T(8,128)(2,1)S(1)}, u32[]{:S(2)}, u32[]{:S(2)}) collective-permute-start(bf16[96,256]{1,0:T(8,128)(2,1)S(1)} %get-tuple-element.22), channel_id=1, source_target_pairs={{0,16},{8,24},{16,0},{24,8},{1,17},{9,25},{17,1},{25,9},{2,18},{10... | collective-permute-start | bytes 147464 | tf_op jit(solution)/shard_map/ppermute | solution.py:26
  14.9 0.0 collective-permute-done.near
  14.9 0.0 collective-permute-start.1
  14.9 2.7 %collective-permute-done.2.half = bf16[96,256]{1,0:T(8,128)(2,1)S(1)} collective-permute-done((bf16[96,256]{1,0:T(8,128)(2,1)S(1)}, bf16[96,256]{1,0:T(8,128)(2,1)S(1)}, u32[]{:S(2)}, u32[]{:S(2)}) %collective-permute-start.2) | collective-permute-done | bytes 49184 | tf_op jit(solution)/shard_map/ppermute | solution.py:26
  17.5 0.0 collective-permute-start.3
  17.5 1.2 %collective-permute-done.3.other = bf16[96,256]{1,0:T(8,128)(2,1)S(1)} collective-permute-done((bf16[96,256]{1,0:T(8,128)(2,1)S(1)}, bf16[96,256]{1,0:T(8,128)(2,1)S(1)}, u32[]{:S(2)}, u32[]{:S(2)}) %collective-permute-start.3) | collective-permute-done | bytes 49184 | tf_op jit(solution)/shard_map/ppermute | solution.py:26
  18.8 0.0 collective-permute-done.1.mated
  18.8 0.7 %shard_map.87 = (bf16[64,2048]{1,0:T(8,128)(2,1)S(1)}, f32[64,1536]{1,0:T(8,128)S(1)}, f32[64,512]{1,0:T(8,128)S(1)}, bf16[64,256]{1,0:T(8,128)(2,1)S(1)}) custom-call(bf16[4,256,256]{2,1,0:T(8,128)(2,1)S(1)} %shard_map.86.picks_ref, bf16[256,2048]{1,0:T(8,128)(2,1)S(1)} %get-tuple-element.19.damage_ref, bf16[256,256]{1,0:T(8,128)(2,1)S(1)} %get-tuple-element.20.own, ...), custom_call_target="tpu_custom_call" | custom-call | flops 1048576 | bytes 1048576 | tf_op jit(solution)/shard_map/pallas_call | solution.py:247
  19.5 1.3 %collective-permute-start.4 = (bf16[64,2048]{1,0:T(8,128)(2,1)S(1)}, bf16[64,2048]{1,0:T(8,128)(2,1)S(1)}, u32[]{:S(2)}, u32[]{:S(2)}) collective-permute-start(bf16[64,2048]{1,0:T(8,128)(2,1)S(1)} %get-tuple-element.24), channel_id=1, source_target_pairs={{0,8},{1,17},{2,10},{3,19},{4,12},{5,21},{6,14},{7,23},{8,0},{9,25... | collective-permute-start | bytes 786440 | tf_op jit(solution)/shard_map/ppermute | solution.py:36
  20.8 0.0 collective-permute-done.9.two_ref
  20.8 1.6 %collective-permute-start.10 = (bf16[64,1536]{1,0:T(8,128)(2,1)S(1)}, bf16[64,1536]{1,0:T(8,128)(2,1)S(1)}, u32[]{:S(2)}, u32[]{:S(2)}) collective-permute-start(bf16[64,1536]{1,0:T(8,128)(2,1)S(1)} %shard_map.90), channel_id=1, source_target_pairs={{0,16},{1,9},{2,18},{3,11},{4,20},{5,13},{6,22},{7,15},{8,24},{9,1... | collective-permute-start | bytes 589832 | tf_op jit(solution)/shard_map/ppermute | solution.py:36
  22.4 0.2 shard_map.91
  22.6 1.1 %collective-permute-start.11 = (bf16[64,512]{1,0:T(8,128)(2,1)S(1)}, bf16[64,512]{1,0:T(8,128)(2,1)S(1)}, u32[]{:S(2)}, u32[]{:S(2)}) collective-permute-start(bf16[64,512]{1,0:T(8,128)(2,1)S(1)} %shard_map.91), channel_id=1, source_target_pairs={{0,8},{1,17},{2,10},{3,19},{4,12},{5,21},{6,14},{7,23},{8,0},{9,25... | collective-permute-start | bytes 196616 | tf_op jit(solution)/shard_map/ppermute | solution.py:36
  23.6 5.1 %collective-permute-done.11.two_ref = bf16[64,512]{1,0:T(8,128)(2,1)S(1)} collective-permute-done((bf16[64,512]{1,0:T(8,128)(2,1)S(1)}, bf16[64,512]{1,0:T(8,128)(2,1)S(1)}, u32[]{:S(2)}, u32[]{:S(2)}) %collective-permute-start.11) | collective-permute-done | bytes 65568 | tf_op jit(solution)/shard_map/ppermute | solution.py:36
  28.7 1.1 %collective-permute-start.12 = (bf16[64,512]{1,0:T(8,128)(2,1)S(1)}, bf16[64,512]{1,0:T(8,128)(2,1)S(1)}, u32[]{:S(2)}, u32[]{:S(2)}) collective-permute-start(bf16[64,512]{1,0:T(8,128)(2,1)S(1)} %shard_map.92), channel_id=1, source_target_pairs={{0,16},{1,9},{2,18},{3,11},{4,20},{5,13},{6,22},{7,15},{8,24},{9,1... | collective-permute-start | bytes 196616 | tf_op jit(solution)/shard_map/ppermute | solution.py:36
  29.9 0.3 shard_map.88.own_ref
  30.2 2.9 %collective-permute-done.12.refs_2_ = bf16[64,512]{1,0:T(8,128)(2,1)S(1)} collective-permute-done((bf16[64,512]{1,0:T(8,128)(2,1)S(1)}, bf16[64,512]{1,0:T(8,128)(2,1)S(1)}, u32[]{:S(2)}, u32[]{:S(2)}) %collective-permute-start.12) | collective-permute-done | bytes 65568 | tf_op jit(solution)/shard_map/ppermute | solution.py:36
  33.1 0.0 collective-permute-done.10.refs_1_
  33.1 0.0 collective-permute-done.4.refs_0_
  33.1 0.3 shard_map.93
  33.3 0.0 collective-permute-start.13
  33.3 1.1 %collective-permute-done.13 = f32[2,64]{1,0:T(2,128)S(1)} collective-permute-done((f32[2,64]{1,0:T(2,128)S(1)}, f32[2,64]{1,0:T(2,128)S(1)}, u32[]{:S(2)}, u32[]{:S(2)}) %collective-permute-start.13) | collective-permute-done | bytes 544 | tf_op jit(solution)/shard_map/ppermute | solution.py:41
  34.5 3.1 %collective-permute-start.15 = (f32[2,64]{1,0:T(2,128)S(1)}, f32[2,64]{1,0:T(2,128)S(1)}, u32[]{:S(2)}, u32[]{:S(2)}) collective-permute-start(f32[2,64]{1,0:T(2,128)S(1)} %pad_maximum_fusion), channel_id=1, source_target_pairs={{0,4},{1,7},{2,6},{3,5},{4,0},{5,3},{6,2},{7,1},{8,12},{9,15},{10,... | collective-permute-start | bytes 1544 | tf_op jit(solution)/shard_map/ppermute | solution.py:41
  37.6 1.6 %collective-permute-start.14 = (f32[2,64]{1,0:T(2,128)S(1)}, f32[2,64]{1,0:T(2,128)S(1)}, u32[]{:S(2)}, u32[]{:S(2)}) collective-permute-start(f32[2,64]{1,0:T(2,128)S(1)} %pad_maximum_fusion), channel_id=1, source_target_pairs={{0,2},{1,3},{2,0},{3,1},{4,6},{5,7},{6,4},{7,5},{8,10},{9,11},{10,... | collective-permute-start | bytes 1544 | tf_op jit(solution)/shard_map/ppermute | solution.py:41
  39.1 0.0 collective-permute-done.15
  39.2 0.3 collective-permute-start.16
  39.4 0.7 %shard_map.94 = bf16[64,2048]{1,0:T(8,128)(2,1)} custom-call(f32[64,2048]{1,0:T(8,128)S(1)} %get-tuple-element.31.values_ref), custom_call_target="tpu_custom_call" | custom-call | flops 1048576 | bytes 1048576 | tf_op jit(solution)/shard_map/pallas_call | solution.py:247
  40.2 1.0 %collective-permute-done.14 = f32[2,64]{1,0:T(2,128)S(1)} collective-permute-done((f32[2,64]{1,0:T(2,128)S(1)}, f32[2,64]{1,0:T(2,128)S(1)}, u32[]{:S(2)}, u32[]{:S(2)}) %collective-permute-start.14) | collective-permute-done | bytes 544 | tf_op jit(solution)/shard_map/ppermute | solution.py:41
  41.2 0.0 collective-permute-done.16
  41.2 0.5 %sqrt_bitcast_fusion = (f32[64]{0:T(128)}, f32[64]{0:T(128)}) fusion(f32[2,64]{1,0:T(2,128)S(1)} %collective-permute-done.16, f32[2,64]{1,0:T(2,128)S(1)} %collective-permute-done.15, f32[1,64]{1,0:T(1,128)S(1)} %get-tuple-element.35, f32[2,64]{1,0:T(2,128)S(1)} %collective-permute-done.14, f32[1,64]{1,0:T(1,128)S(1)} %get-tuple-element.36), kind=kLoop, calls=%fused_computation.1 | loop fusion | flops 512 | bytes 2560 | tf_op jit(solution)/shard_map/sqrt | solution.py:357
  (4 shorter events, 0.1 us)
Async XLA Ops:
  2.6 5.1 %collective-permute-start.5 = (bf16[64,256]{1,0:T(8,128)(2,1)S(1)}, bf16[64,256]{1,0:T(8,128)(2,1)S(1)}, u32[]{:S(2)}, u32[]{:S(2)}) collective-permute-start(bf16[64,256]{1,0:T(8,128)(2,1)S(1)} %get-tuple-element.26), channel_id=1, source_target_pairs={{0,8},{1,25},{2,10},{3,27},{4,12},{5,29},{6,14},{7,31},{8,0},{9,17... | collective-permute-start | bytes 98312 | tf_op jit(solution)/shard_map/ppermute | solution.py:36
  5.6 9.3 %collective-permute-start = (bf16[192,256]{1,0:T(8,128)(2,1)S(1)}, bf16[192,256]{1,0:T(8,128)(2,1)S(1)}, u32[]{:S(2)}, u32[]{:S(2)}) collective-permute-start(bf16[192,256]{1,0:T(8,128)(2,1)S(1)} %get-tuple-element.21), channel_id=1, source_target_pairs={{0,8},{1,25},{2,10},{3,27},{4,12},{5,29},{6,14},{7,31},{8,0},{9,17... | collective-permute-start | bytes 294920 | tf_op jit(solution)/shard_map/ppermute | solution.py:36
  5.7 3.7 %collective-permute-start.7 = (bf16[32,256]{1,0:T(8,128)(2,1)S(1)}, bf16[32,256]{1,0:T(8,128)(2,1)S(1)}, u32[]{:S(2)}, u32[]{:S(2)}) collective-permute-start(bf16[32,256]{1,0:T(8,128)(2,1)S(1)} %get-tuple-element.27), channel_id=1, source_target_pairs={{0,16},{8,24},{16,0},{24,8},{1,17},{9,25},{17,1},{25,9},{2,18},{10... | collective-permute-start | bytes 49160 | tf_op jit(solution)/shard_map/ppermute | solution.py:26
  7.6 3.0 %collective-permute-start.6 = (bf16[64,256]{1,0:T(8,128)(2,1)S(1)}, bf16[64,256]{1,0:T(8,128)(2,1)S(1)}, u32[]{:S(2)}, u32[]{:S(2)}) collective-permute-start(bf16[64,256]{1,0:T(8,128)(2,1)S(1)} %collective-permute-done.5.near), channel_id=1, source_target_pairs={{0,1},{1,0},{2,3},{3,2},{4,5},{5,4},{6,7},{7,6},{8,9},{9,8},{10,11... | collective-permute-start | bytes 98312 | tf_op jit(solution)/shard_map/ppermute | solution.py:26
  9.4 1.2 %collective-permute-start.8 = (bf16[32,256]{1,0:T(8,128)(2,1)S(1)}, bf16[32,256]{1,0:T(8,128)(2,1)S(1)}, u32[]{:S(2)}, u32[]{:S(2)}) collective-permute-start(bf16[32,256]{1,0:T(8,128)(2,1)S(1)} %collective-permute-done.7.half), channel_id=1, source_target_pairs={{0,1},{1,0},{2,3},{3,2},{4,5},{5,4},{6,7},{7,6},{8,9},{9,8},{10,11... | collective-permute-start | bytes 49160 | tf_op jit(solution)/shard_map/ppermute | solution.py:26
  11.2 9.6 %collective-permute-start.9 = (bf16[64,1536]{1,0:T(8,128)(2,1)S(1)}, bf16[64,1536]{1,0:T(8,128)(2,1)S(1)}, u32[]{:S(2)}, u32[]{:S(2)}) collective-permute-start(bf16[64,1536]{1,0:T(8,128)(2,1)S(1)} %get-tuple-element.28), channel_id=1, source_target_pairs={{0,8},{1,17},{2,10},{3,19},{4,12},{5,21},{6,14},{7,23},{8,0},{9,25... | collective-permute-start | bytes 589832 | tf_op jit(solution)/shard_map/ppermute | solution.py:36
  13.3 4.2 %collective-permute-start.2 = (bf16[96,256]{1,0:T(8,128)(2,1)S(1)}, bf16[96,256]{1,0:T(8,128)(2,1)S(1)}, u32[]{:S(2)}, u32[]{:S(2)}) collective-permute-start(bf16[96,256]{1,0:T(8,128)(2,1)S(1)} %get-tuple-element.22), channel_id=1, source_target_pairs={{0,16},{8,24},{16,0},{24,8},{1,17},{9,25},{17,1},{25,9},{2,18},{10... | collective-permute-start | bytes 147464 | tf_op jit(solution)/shard_map/ppermute | solution.py:26
  14.9 3.9 %collective-permute-start.1 = (bf16[192,256]{1,0:T(8,128)(2,1)S(1)}, bf16[192,256]{1,0:T(8,128)(2,1)S(1)}, u32[]{:S(2)}, u32[]{:S(2)}) collective-permute-start(bf16[192,256]{1,0:T(8,128)(2,1)S(1)} %collective-permute-done.near), channel_id=1, source_target_pairs={{0,1},{1,0},{2,3},{3,2},{4,5},{5,4},{6,7},{7,6},{8,9},{9,8},{10,11... | collective-permute-start | bytes 294920 | tf_op jit(solution)/shard_map/ppermute | solution.py:26
  17.5 1.2 %collective-permute-start.3 = (bf16[96,256]{1,0:T(8,128)(2,1)S(1)}, bf16[96,256]{1,0:T(8,128)(2,1)S(1)}, u32[]{:S(2)}, u32[]{:S(2)}) collective-permute-start(bf16[96,256]{1,0:T(8,128)(2,1)S(1)} %collective-permute-done.2.half), channel_id=1, source_target_pairs={{0,1},{1,0},{2,3},{3,2},{4,5},{5,4},{6,7},{7,6},{8,9},{9,8},{10,11... | collective-permute-start | bytes 147464 | tf_op jit(solution)/shard_map/ppermute | solution.py:26
  19.5 13.6 %collective-permute-start.4 = (bf16[64,2048]{1,0:T(8,128)(2,1)S(1)}, bf16[64,2048]{1,0:T(8,128)(2,1)S(1)}, u32[]{:S(2)}, u32[]{:S(2)}) collective-permute-start(bf16[64,2048]{1,0:T(8,128)(2,1)S(1)} %get-tuple-element.24), channel_id=1, source_target_pairs={{0,8},{1,17},{2,10},{3,19},{4,12},{5,21},{6,14},{7,23},{8,0},{9,25... | collective-permute-start | bytes 786440 | tf_op jit(solution)/shard_map/ppermute | solution.py:36
  20.8 12.3 %collective-permute-start.10 = (bf16[64,1536]{1,0:T(8,128)(2,1)S(1)}, bf16[64,1536]{1,0:T(8,128)(2,1)S(1)}, u32[]{:S(2)}, u32[]{:S(2)}) collective-permute-start(bf16[64,1536]{1,0:T(8,128)(2,1)S(1)} %shard_map.90), channel_id=1, source_target_pairs={{0,16},{1,9},{2,18},{3,11},{4,20},{5,13},{6,22},{7,15},{8,24},{9,1... | collective-permute-start | bytes 589832 | tf_op jit(solution)/shard_map/ppermute | solution.py:36
  22.6 6.2 %collective-permute-start.11 = (bf16[64,512]{1,0:T(8,128)(2,1)S(1)}, bf16[64,512]{1,0:T(8,128)(2,1)S(1)}, u32[]{:S(2)}, u32[]{:S(2)}) collective-permute-start(bf16[64,512]{1,0:T(8,128)(2,1)S(1)} %shard_map.91), channel_id=1, source_target_pairs={{0,8},{1,17},{2,10},{3,19},{4,12},{5,21},{6,14},{7,23},{8,0},{9,25... | collective-permute-start | bytes 196616 | tf_op jit(solution)/shard_map/ppermute | solution.py:36
  28.7 4.3 %collective-permute-start.12 = (bf16[64,512]{1,0:T(8,128)(2,1)S(1)}, bf16[64,512]{1,0:T(8,128)(2,1)S(1)}, u32[]{:S(2)}, u32[]{:S(2)}) collective-permute-start(bf16[64,512]{1,0:T(8,128)(2,1)S(1)} %shard_map.92), channel_id=1, source_target_pairs={{0,16},{1,9},{2,18},{3,11},{4,20},{5,13},{6,22},{7,15},{8,24},{9,1... | collective-permute-start | bytes 196616 | tf_op jit(solution)/shard_map/ppermute | solution.py:36
  33.3 1.2 %collective-permute-start.13 = (f32[2,64]{1,0:T(2,128)S(1)}, f32[2,64]{1,0:T(2,128)S(1)}, u32[]{:S(2)}, u32[]{:S(2)}) collective-permute-start(f32[2,64]{1,0:T(2,128)S(1)} %get-tuple-element.32), channel_id=1, source_target_pairs={{0,1},{1,0},{2,3},{3,2},{4,5},{5,4},{6,7},{7,6},{8,9},{9,8},{10,11... | collective-permute-start | bytes 1544 | tf_op jit(solution)/shard_map/ppermute | solution.py:41
  34.5 4.6 %collective-permute-start.15 = (f32[2,64]{1,0:T(2,128)S(1)}, f32[2,64]{1,0:T(2,128)S(1)}, u32[]{:S(2)}, u32[]{:S(2)}) collective-permute-start(f32[2,64]{1,0:T(2,128)S(1)} %pad_maximum_fusion), channel_id=1, source_target_pairs={{0,4},{1,7},{2,6},{3,5},{4,0},{5,3},{6,2},{7,1},{8,12},{9,15},{10,... | collective-permute-start | bytes 1544 | tf_op jit(solution)/shard_map/ppermute | solution.py:41
  37.6 3.6 %collective-permute-start.14 = (f32[2,64]{1,0:T(2,128)S(1)}, f32[2,64]{1,0:T(2,128)S(1)}, u32[]{:S(2)}, u32[]{:S(2)}) collective-permute-start(f32[2,64]{1,0:T(2,128)S(1)} %pad_maximum_fusion), channel_id=1, source_target_pairs={{0,2},{1,3},{2,0},{3,1},{4,6},{5,7},{6,4},{7,5},{8,10},{9,11},{10,... | collective-permute-start | bytes 1544 | tf_op jit(solution)/shard_map/ppermute | solution.py:41
  39.2 2.0 %collective-permute-start.16 = (f32[2,64]{1,0:T(2,128)S(1)}, f32[2,64]{1,0:T(2,128)S(1)}, u32[]{:S(2)}, u32[]{:S(2)}) collective-permute-start(f32[2,64]{1,0:T(2,128)S(1)} %collective-permute-done.15), channel_id=1, source_target_pairs={{0,1},{1,0},{2,3},{3,2},{4,5},{5,4},{6,7},{7,6},{8,9},{9,8},{10,11... | collective-permute-start | bytes 1544 | tf_op jit(solution)/shard_map/ppermute | solution.py:41

commit v4 on v3

--- a/solution.py
+++ b/solution.py
@@ -79,19 +79,16 @@
         odd = lax.axis_index("node") % 2
         near_head, near_tail, side_head, side_tail = sends
         per_group = near_head.shape[0]
-        other = me ^ (1 + 2 * odd)
+        other = me ^ (2 + odd)
         near_head[...] = rows_of(scores, other ^ 3, per_group)
         for place, step in enumerate((1, 2, 0)):
             near_tail[place * per_group : (place + 1) * per_group, :] = rows_of(
                 scores, other ^ step, per_group
             )
-        small = per_group // 2
-        side_head[...] = rows_of(scores, (me ^ 1) * 2 + odd, small)
-        for place in range(3):
-            piece = odd * 3 + place
-            step = jnp.where(piece // 2 == 0, 1, jnp.where(piece // 2 == 1, 2, 0))
-            side_tail[place * small : (place + 1) * small, :] = rows_of(
-                scores, (me ^ 2 ^ step) * 2 + piece % 2, small
+        side_head[...] = rows_of(scores, me ^ 2, per_group)
+        for place, step in enumerate((1, 2, 0)):
+            side_tail[place * per_group : (place + 1) * per_group, :] = rows_of(
+                scores, me ^ 1 ^ step, per_group
             )
     copies[4].wait()
     live = lax.broadcasted_iota(jnp.int32, named.shape, 1) < counts[me]
@@ -109,13 +106,6 @@
     for step in range(groups):
         first = origin(me, step, groups) * out_ref.shape[1]
         out_ref[step] = jnp.where(row == named_ref[...] - first, 1.0, 0.0).astype(out_ref.dtype)
-
-
-def join(half_ref, other_ref, joined):
-    odd = lax.axis_index("node") % 2
-    rows = half_ref.shape[0]
-    joined[pl.ds(pl.multiple_of(odd * rows, rows), rows), :] = half_ref[...]
-    joined[pl.ds(pl.multiple_of((1 - odd) * rows, rows), rows), :] = other_ref[...]
 
 
 def project(weight, damage_ref, start, outs, tile):
@@ -130,15 +120,14 @@
             out[:, at : at + tile] = part[k * rows : (k + 1) * rows, :].astype(out.dtype)
 
 
-def first_kernel(tile, picks_ref, damage_ref, own, near, mated, half, other, weight, out, joined):
+def first_kernel(tile, picks_ref, damage_ref, own, near, mated, side, weight, out):
     odd = lax.axis_index("node") % 2
-    join(half, other, joined)
     total = jnp.dot(
         rows_of(own, lax.axis_index("grp") ^ 3, near.shape[0]),
         picks_ref[0],
         preferred_element_type=jnp.float32,
     )
-    for ref, step in ((near, 1 + 2 * odd), (mated, 3 - 2 * odd), (joined, 2)):
+    for ref, step in ((near, 2 + odd), (mated, 3 - odd), (side, 1)):
         total += jnp.dot(ref[...], picks_ref[step], preferred_element_type=jnp.float32)
     weight[...] = total.astype(weight.dtype)
     project(weight[...], damage_ref, 0, [out], tile)
@@ -148,17 +137,16 @@
     project(weight_ref[...], damage_ref, damage_ref.shape[1] - out_ref.shape[1], [out_ref], tile)
 
 
-def other_kernel(tile, picks_ref, damage_ref, own, near, mated, half, other, *refs):
-    sent, kept, later, weight, order, joined = refs
+def other_kernel(tile, picks_ref, damage_ref, own, near, mated, side, *refs):
+    sent, kept, later, weight, order = refs
     odd = lax.axis_index("node") % 2
     me = lax.axis_index("grp")
-    join(half, other, joined)
     rows = sent.shape[0]
-    steps = (1 + odd, 2 - odd, 0)
+    steps = (2 - odd, 1 + odd, 0)
     total = None
-    for ref, step in ((own, 0), (near, 1 + 2 * odd), (mated, 3 - 2 * odd), (joined, 2)):
+    for ref, step in ((own, 0), (near, 2 + odd), (mated, 3 - odd), (side, 1)):
         for place, target in enumerate(steps):
-            block = me ^ target if ref is own else (odd, 1 - odd, 2)[place]
+            block = me ^ target if ref is own else (1 - odd, odd, 2)[place]
             order[place * rows : (place + 1) * rows, :] = rows_of(ref, block, rows)
         part = jnp.dot(order[...], picks_ref[step], preferred_element_type=jnp.float32)
         total = part if total is None else total + part
@@ -266,7 +254,7 @@
     paired = is_paired(groups, nodes)
     operands = (new_table, new_ids.reshape(1, samples), basis_table, train_ids.reshape(1, slots), counts, damage)
     rest = samples - per_group
-    sends = [(per_group, rows), (rest, rows), (per_group // 2, rows), (rest // 2, rows)]
+    sends = [(per_group, rows), (rest, rows)] * 2
     scores, named, damage, *sends = call(
         functools.partial(scores_kernel, groups),
         [((samples, rows), half), ((1, slots), jnp.int32), ((slots, cells), half)]
@@ -294,40 +282,39 @@
         tile = math.gcd(512, *widths)
         pieces = [(per_group, width) for width in widths]
         near_head, near_tail, side_head, side_tail = sends
-        side_head = swap(side_head, "grp", 2)
-        near_head = split_swap(near_head, (1, 3))
-        side_tail = swap(side_tail, "grp", 2)
-        near_tail = split_swap(near_tail, (1, 3))
-        heads = (near_head, swap(near_head, "node", 1), side_head, swap(side_head, "node", 1))
-        tails = (near_tail, swap(near_tail, "node", 1), side_tail, swap(side_tail, "node", 1))
+        side_head = swap(side_head, "grp", 1)
+        near_head = split_swap(near_head, (2, 3))
+        side_tail = swap(side_tail, "grp", 1)
+        near_tail = split_swap(near_tail, (2, 3))
+        heads = (near_head, swap(near_head, "node", 1), side_head)
+        tails = (near_tail, swap(near_tail, "node", 1), side_tail)
         weight, first = call(
             functools.partial(first_kernel, tile),
             [((per_group, slots), half), (pieces[0], half)],
-            [FULL] * 7,
+            [FULL] * 6,
             picks,
             damage,
             scores,
             *heads,
-            scratch=[pltpu.VMEM((per_group, rows), half)],
         )
         second = call(
             functools.partial(second_kernel, tile), [(pieces[1], half)], [FULL] * 2, weight, damage
         )[0]
-        passed = [split_swap(x, (1, 2)) for x in (first, second)]
+        passed = [split_swap(x, (2, 1)) for x in (first, second)]
         sent, *kept, weight = call(
             functools.partial(other_kernel, tile),
             [part, (pieces[0], full), (pieces[1], full), ((per_group, slots), half)],
-            [FULL] * 7,
+            [FULL] * 6,
             picks,
             damage,
             scores,
             *tails,
-            scratch=[pltpu.VMEM((rest, rows), half)] * 2,
+            scratch=[pltpu.VMEM((rest, rows), half)],
         )
-        arrived = [split_swap(sent, (1, 2))]
+        arrived = [split_swap(sent, (2, 1))]
         for k in range(2):
             both = call(add_kernel, [(pieces[k], half)], [FULL] * 2, kept[k], passed[k])[0]
-            arrived.append(split_swap(both, (2, 1)))
+            arrived.append(split_swap(both, (1, 2)))
         own = call(
             functools.partial(own_kernel, tile), [((per_group, cells), full)], [FULL] * 2, weight, damage
         )[0]
@@ -359,7 +346,7 @@
 
 
 def split_columns(cells):
-    late = cells // 4
+    late = 3 * cells // 8
     return cells - late, late
 
 

time: 41.9 us -> 39.2 us (0.936)
  waiting for transfers between devices: 16.9 us -> 12.3 us
  starting transfers between devices: 18.8 us -> 20.6 us
    ppermute x6 -> x4, waiting for transfers between devices: 6.74 us -> 1 us  [swap(): lax.ppermute(value, axis, [(i, mate(i, step, size)) for i in range(size)])]
    ppermute x7, starting transfers between devices: 10.4 us -> 12.1 us  [split_swap(): return lax.ppermute(value, ('grp', 'node'), pairs)]
    ppermute x7, waiting for transfers between devices: 7.99 us -> 8.93 us  [split_swap(): return lax.ppermute(value, ('grp', 'node'), pairs)]
    ppermute x6 -> x4, starting transfers between devices: 3.51 us -> 4.24 us  [swap(): lax.ppermute(value, axis, [(i, mate(i, step, size)) for i in range(size)])]
    ppermute x4, starting transfers between devices: 4.94 us -> 4.26 us  [node_swap(): return lax.ppermute(value, 'node', pairs)]
  transfers between devices with their start and end apart: 17 -> 15, of which waited for: 8 -> 7; matrix products, arithmetic and copies ran while one was open for 0% -> 0% of each run, Pallas kernels for 6% -> 7%
where the time goes in v4:
time: 39.2 us; the launch traced here: 39 us
  starting transfers between devices  20.6 us (53%)
  waiting for transfers between devices  12.3 us (31%)
  Pallas kernels  4.78 us (12%)
  between operations  0.7 us (2%)
  other arithmetic  0.54 us (1%)
    ppermute x7, starting transfers between devices, split_swap(): return lax.ppermute(value, ('grp', 'node'), pairs)  12.1 us
    ppermute x7, waiting for transfers between devices, split_swap(): return lax.ppermute(value, ('grp', 'node'), pairs)  8.93 us
    pallas_call x10, Pallas kernels, call(): pl.pallas_call(kernel, out_shape=[jax.ShapeDtypeStruct(shape, kind) for s...  4.78 us
    ppermute x4, starting transfers between devices, node_swap(): return lax.ppermute(value, 'node', pairs)  4.26 us
    ppermute x4, starting transfers between devices, swap(): lax.ppermute(value, axis, [(i, mate(i, step, size)) for i in range(size)])  4.24 us
    ppermute x4, waiting for transfers between devices, node_swap(): return lax.ppermute(value, 'node', pairs)  2.41 us
    ppermute x4, waiting for transfers between devices, swap(): lax.ppermute(value, axis, [(i, mate(i, step, size)) for i in range(size)])  1 us
  transfers between devices with their start and end apart: 15, of which 7 were waited for; matrix products, arithmetic and copies ran while one was open for 0% of the time, Pallas kernels for 7%

profile of v4, /device:TPU:0, one launch (start us, length us, event | category | flops | bytes accessed | tf_op | source)
XLA Modules:
  0.0 39.0 jit_solution(306606699173712521)
XLA Ops:
  0.6 1.9 %shard_map.85 = (bf16[256,256]{1,0:T(8,128)(2,1)S(1)}, s32[1,256]{1,0:T(1,128)S(1)}, bf16[256,2048]{1,0:T(8,128)(2,1)S(1)}, bf16[64,256]{1,0:T(8,128)(2,1)S(1)},...) custom-call(bf16[512,512]{1,0:T(8,128)(2,1)} %table_ref.1, ...), custom_call_target="tpu_custom_call" | custom-call | flops 1048576 | bytes 1048576 | tf_op jit(solution)/shard_map/pallas_call | solution.py:235
  2.6 3.1 %collective-permute-start = (bf16[192,256]{1,0:T(8,128)(2,1)S(1)}, bf16[192,256]{1,0:T(8,128)(2,1)S(1)}, u32[]{:S(2)}, u32[]{:S(2)}) collective-permute-start(bf16[192,256]{1,0:T(8,128)(2,1)S(1)} %get-tuple-element.21), channel_id=1, source_target_pairs={{0,16},{1,25},{2,18},{3,27},{4,20},{5,29},{6,22},{7,31},{8,24},{9,... | collective-permute-start | bytes 294920 | tf_op jit(solution)/shard_map/ppermute | solution.py:36
  5.6 0.1 collective-permute-start.4
  5.7 1.9 %collective-permute-start.6 = (bf16[64,256]{1,0:T(8,128)(2,1)S(1)}, bf16[64,256]{1,0:T(8,128)(2,1)S(1)}, u32[]{:S(2)}, u32[]{:S(2)}) collective-permute-start(bf16[64,256]{1,0:T(8,128)(2,1)S(1)} %get-tuple-element.27), channel_id=1, source_target_pairs={{0,8},{8,0},{16,24},{24,16},{1,9},{9,1},{17,25},{25,17},{2,10},{10... | collective-permute-start | bytes 98312 | tf_op jit(solution)/shard_map/ppermute | solution.py:26
  7.6 2.0 %collective-permute-done.4.near = bf16[64,256]{1,0:T(8,128)(2,1)S(1)} collective-permute-done((bf16[64,256]{1,0:T(8,128)(2,1)S(1)}, bf16[64,256]{1,0:T(8,128)(2,1)S(1)}, u32[]{:S(2)}, u32[]{:S(2)}) %collective-permute-start.4) | collective-permute-done | bytes 32800 | tf_op jit(solution)/shard_map/ppermute | solution.py:36
  9.6 0.2 collective-permute-start.5
  9.8 1.9 %collective-permute-start.2 = (bf16[192,256]{1,0:T(8,128)(2,1)S(1)}, bf16[192,256]{1,0:T(8,128)(2,1)S(1)}, u32[]{:S(2)}, u32[]{:S(2)}) collective-permute-start(bf16[192,256]{1,0:T(8,128)(2,1)S(1)} %get-tuple-element.22), channel_id=1, source_target_pairs={{0,8},{8,0},{16,24},{24,16},{1,9},{9,1},{17,25},{25,17},{2,10},{10... | collective-permute-start | bytes 294920 | tf_op jit(solution)/shard_map/ppermute | solution.py:26
  11.7 0.0 collective-permute-done.near
  11.7 0.2 collective-permute-start.1
  12.0 0.1 shard_map.86.picks_ref
  12.1 0.0 collective-permute-done.6.side
  12.1 0.0 collective-permute-done.5.mated
  12.1 0.5 %shard_map.89 = (bf16[64,256]{1,0:T(8,128)(2,1)S(1)}, bf16[64,1280]{1,0:T(8,128)(2,1)S(1)}) custom-call(bf16[4,256,256]{2,1,0:T(8,128)(2,1)S(1)} %shard_map.86.picks_ref, bf16[256,2048]{1,0:T(8,128)(2,1)S(1)} %get-tuple-element.19.damage_ref, bf16[256,256]{1,0:T(8,128)(2,1)S(1)} %get-tuple-element.20.own, bf16[64,256]{1,0:T(8,128)(2,1)S(1)} %collective-permute-done.4.near, ...), custom_call_target="tpu_custom_call" | custom-call | flops 1048576 | bytes 1048576 | tf_op jit(solution)/shard_map/pallas_call | solution.py:235
  12.6 1.6 %collective-permute-start.7 = (bf16[64,1280]{1,0:T(8,128)(2,1)S(1)}, bf16[64,1280]{1,0:T(8,128)(2,1)S(1)}, u32[]{:S(2)}, u32[]{:S(2)}) collective-permute-start(bf16[64,1280]{1,0:T(8,128)(2,1)S(1)} %get-tuple-element.28), channel_id=1, source_target_pairs={{0,16},{1,9},{2,18},{3,11},{4,20},{5,13},{6,22},{7,15},{8,24},{9,1... | collective-permute-start | bytes 491528 | tf_op jit(solution)/shard_map/ppermute | solution.py:36
  14.2 1.0 %collective-permute-done.2.side = bf16[192,256]{1,0:T(8,128)(2,1)S(1)} collective-permute-done((bf16[192,256]{1,0:T(8,128)(2,1)S(1)}, bf16[192,256]{1,0:T(8,128)(2,1)S(1)}, u32[]{:S(2)}, u32[]{:S(2)}) %collective-permute-start.2) | collective-permute-done | bytes 98336 | tf_op jit(solution)/shard_map/ppermute | solution.py:26
  15.2 0.0 collective-permute-done.1.mated
  15.2 0.7 %shard_map.87 = (bf16[64,2048]{1,0:T(8,128)(2,1)S(1)}, f32[64,1280]{1,0:T(8,128)S(1)}, f32[64,768]{1,0:T(8,128)S(1)}, bf16[64,256]{1,0:T(8,128)(2,1)S(1)}) custom-call(bf16[4,256,256]{2,1,0:T(8,128)(2,1)S(1)} %shard_map.86.picks_ref, bf16[256,2048]{1,0:T(8,128)(2,1)S(1)} %get-tuple-element.19.damage_ref, bf16[256,256]{1,0:T(8,128)(2,1)S(1)} %get-tuple-element.20.own, ...), custom_call_target="tpu_custom_call" | custom-call | flops 1048576 | bytes 1048576 | tf_op jit(solution)/shard_map/pallas_call | solution.py:235
  15.9 1.8 %collective-permute-start.3 = (bf16[64,2048]{1,0:T(8,128)(2,1)S(1)}, bf16[64,2048]{1,0:T(8,128)(2,1)S(1)}, u32[]{:S(2)}, u32[]{:S(2)}) collective-permute-start(bf16[64,2048]{1,0:T(8,128)(2,1)S(1)} %get-tuple-element.24), channel_id=1, source_target_pairs={{0,16},{1,9},{2,18},{3,11},{4,20},{5,13},{6,22},{7,15},{8,24},{9,1... | collective-permute-start | bytes 786440 | tf_op jit(solution)/shard_map/ppermute | solution.py:36
  17.7 0.2 shard_map.91
  17.9 0.3 collective-permute-start.9
  18.2 0.0 collective-permute-done.7.two_ref
  18.3 2.3 %collective-permute-start.8 = (bf16[64,1280]{1,0:T(8,128)(2,1)S(1)}, bf16[64,1280]{1,0:T(8,128)(2,1)S(1)}, u32[]{:S(2)}, u32[]{:S(2)}) collective-permute-start(bf16[64,1280]{1,0:T(8,128)(2,1)S(1)} %shard_map.90), channel_id=1, source_target_pairs={{0,8},{1,17},{2,10},{3,19},{4,12},{5,21},{6,14},{7,23},{8,0},{9,25... | collective-permute-start | bytes 491528 | tf_op jit(solution)/shard_map/ppermute | solution.py:36
  20.5 4.6 %collective-permute-done.9.two_ref = bf16[64,768]{1,0:T(8,128)(2,1)S(1)} collective-permute-done((bf16[64,768]{1,0:T(8,128)(2,1)S(1)}, bf16[64,768]{1,0:T(8,128)(2,1)S(1)}, u32[]{:S(2)}, u32[]{:S(2)}) %collective-permute-start.9) | collective-permute-done | bytes 98336 | tf_op jit(solution)/shard_map/ppermute | solution.py:36
  25.2 3.0 %collective-permute-start.10 = (bf16[64,768]{1,0:T(8,128)(2,1)S(1)}, bf16[64,768]{1,0:T(8,128)(2,1)S(1)}, u32[]{:S(2)}, u32[]{:S(2)}) collective-permute-start(bf16[64,768]{1,0:T(8,128)(2,1)S(1)} %shard_map.92), channel_id=1, source_target_pairs={{0,8},{1,17},{2,10},{3,19},{4,12},{5,21},{6,14},{7,23},{8,0},{9,25... | collective-permute-start | bytes 294920 | tf_op jit(solution)/shard_map/ppermute | solution.py:36
  28.2 0.3 shard_map.88.own_ref
  28.5 2.3 %collective-permute-done.10.refs_2_ = bf16[64,768]{1,0:T(8,128)(2,1)S(1)} collective-permute-done((bf16[64,768]{1,0:T(8,128)(2,1)S(1)}, bf16[64,768]{1,0:T(8,128)(2,1)S(1)}, u32[]{:S(2)}, u32[]{:S(2)}) %collective-permute-start.10) | collective-permute-done | bytes 98336 | tf_op jit(solution)/shard_map/ppermute | solution.py:36
  30.8 0.0 collective-permute-done.8.refs_1_
  30.8 0.0 collective-permute-done.3.refs_0_
  30.8 0.3 shard_map.93
  31.0 0.0 collective-permute-start.11
  31.1 1.1 %collective-permute-done.11 = f32[2,64]{1,0:T(2,128)S(1)} collective-permute-done((f32[2,64]{1,0:T(2,128)S(1)}, f32[2,64]{1,0:T(2,128)S(1)}, u32[]{:S(2)}, u32[]{:S(2)}) %collective-permute-start.11) | collective-permute-done | bytes 544 | tf_op jit(solution)/shard_map/ppermute | solution.py:41
  32.2 2.7 %collective-permute-start.13 = (f32[2,64]{1,0:T(2,128)S(1)}, f32[2,64]{1,0:T(2,128)S(1)}, u32[]{:S(2)}, u32[]{:S(2)}) collective-permute-start(f32[2,64]{1,0:T(2,128)S(1)} %pad_maximum_fusion), channel_id=1, source_target_pairs={{0,4},{1,7},{2,6},{3,5},{4,0},{5,3},{6,2},{7,1},{8,12},{9,15},{10,... | collective-permute-start | bytes 1544 | tf_op jit(solution)/shard_map/ppermute | solution.py:41
  34.9 1.6 %collective-permute-start.12 = (f32[2,64]{1,0:T(2,128)S(1)}, f32[2,64]{1,0:T(2,128)S(1)}, u32[]{:S(2)}, u32[]{:S(2)}) collective-permute-start(f32[2,64]{1,0:T(2,128)S(1)} %pad_maximum_fusion), channel_id=1, source_target_pairs={{0,2},{1,3},{2,0},{3,1},{4,6},{5,7},{6,4},{7,5},{8,10},{9,11},{10,... | collective-permute-start | bytes 1544 | tf_op jit(solution)/shard_map/ppermute | solution.py:41
  36.5 0.3 collective-permute-done.13
  36.8 0.0 collective-permute-start.14
  36.8 0.7 %shard_map.94 = bf16[64,2048]{1,0:T(8,128)(2,1)} custom-call(f32[64,2048]{1,0:T(8,128)S(1)} %get-tuple-element.31.values_ref), custom_call_target="tpu_custom_call" | custom-call | flops 1048576 | bytes 1048576 | tf_op jit(solution)/shard_map/pallas_call | solution.py:235
  37.5 1.0 %collective-permute-done.12 = f32[2,64]{1,0:T(2,128)S(1)} collective-permute-done((f32[2,64]{1,0:T(2,128)S(1)}, f32[2,64]{1,0:T(2,128)S(1)}, u32[]{:S(2)}, u32[]{:S(2)}) %collective-permute-start.12) | collective-permute-done | bytes 544 | tf_op jit(solution)/shard_map/ppermute | solution.py:41
  38.5 0.0 collective-permute-done.14
  38.5 0.5 %sqrt_bitcast_fusion = (f32[64]{0:T(128)}, f32[64]{0:T(128)}) fusion(f32[2,64]{1,0:T(2,128)S(1)} %collective-permute-done.14, f32[2,64]{1,0:T(2,128)S(1)} %collective-permute-done.13, f32[1,64]{1,0:T(1,128)S(1)} %get-tuple-element.35, f32[2,64]{1,0:T(2,128)S(1)} %collective-permute-done.12, f32[1,64]{1,0:T(1,128)S(1)} %get-tuple-element.36), kind=kLoop, calls=%fused_computation.1 | loop fusion | flops 512 | bytes 2560 | tf_op jit(solution)/shard_map/sqrt | solution.py:344
  (4 shorter events, 0.1 us)
Async XLA Ops:
  2.6 9.2 %collective-permute-start = (bf16[192,256]{1,0:T(8,128)(2,1)S(1)}, bf16[192,256]{1,0:T(8,128)(2,1)S(1)}, u32[]{:S(2)}, u32[]{:S(2)}) collective-permute-start(bf16[192,256]{1,0:T(8,128)(2,1)S(1)} %get-tuple-element.21), channel_id=1, source_target_pairs={{0,16},{1,25},{2,18},{3,27},{4,20},{5,29},{6,22},{7,31},{8,24},{9,... | collective-permute-start | bytes 294920 | tf_op jit(solution)/shard_map/ppermute | solution.py:36
  5.6 4.0 %collective-permute-start.4 = (bf16[64,256]{1,0:T(8,128)(2,1)S(1)}, bf16[64,256]{1,0:T(8,128)(2,1)S(1)}, u32[]{:S(2)}, u32[]{:S(2)}) collective-permute-start(bf16[64,256]{1,0:T(8,128)(2,1)S(1)} %get-tuple-element.26), channel_id=1, source_target_pairs={{0,16},{1,25},{2,18},{3,27},{4,20},{5,29},{6,22},{7,31},{8,24},{9,... | collective-permute-start | bytes 98312 | tf_op jit(solution)/shard_map/ppermute | solution.py:36
  5.7 6.4 %collective-permute-start.6 = (bf16[64,256]{1,0:T(8,128)(2,1)S(1)}, bf16[64,256]{1,0:T(8,128)(2,1)S(1)}, u32[]{:S(2)}, u32[]{:S(2)}) collective-permute-start(bf16[64,256]{1,0:T(8,128)(2,1)S(1)} %get-tuple-element.27), channel_id=1, source_target_pairs={{0,8},{8,0},{16,24},{24,16},{1,9},{9,1},{17,25},{25,17},{2,10},{10... | collective-permute-start | bytes 98312 | tf_op jit(solution)/shard_map/ppermute | solution.py:26
  9.6 2.4 %collective-permute-start.5 = (bf16[64,256]{1,0:T(8,128)(2,1)S(1)}, bf16[64,256]{1,0:T(8,128)(2,1)S(1)}, u32[]{:S(2)}, u32[]{:S(2)}) collective-permute-start(bf16[64,256]{1,0:T(8,128)(2,1)S(1)} %collective-permute-done.4.near), channel_id=1, source_target_pairs={{0,1},{1,0},{2,3},{3,2},{4,5},{5,4},{6,7},{7,6},{8,9},{9,8},{10,11... | collective-permute-start | bytes 98312 | tf_op jit(solution)/shard_map/ppermute | solution.py:26
  9.8 5.4 %collective-permute-start.2 = (bf16[192,256]{1,0:T(8,128)(2,1)S(1)}, bf16[192,256]{1,0:T(8,128)(2,1)S(1)}, u32[]{:S(2)}, u32[]{:S(2)}) collective-permute-start(bf16[192,256]{1,0:T(8,128)(2,1)S(1)} %get-tuple-element.22), channel_id=1, source_target_pairs={{0,8},{8,0},{16,24},{24,16},{1,9},{9,1},{17,25},{25,17},{2,10},{10... | collective-permute-start | bytes 294920 | tf_op jit(solution)/shard_map/ppermute | solution.py:26
  11.7 3.5 %collective-permute-start.1 = (bf16[192,256]{1,0:T(8,128)(2,1)S(1)}, bf16[192,256]{1,0:T(8,128)(2,1)S(1)}, u32[]{:S(2)}, u32[]{:S(2)}) collective-permute-start(bf16[192,256]{1,0:T(8,128)(2,1)S(1)} %collective-permute-done.near), channel_id=1, source_target_pairs={{0,1},{1,0},{2,3},{3,2},{4,5},{5,4},{6,7},{7,6},{8,9},{9,8},{10,11... | collective-permute-start | bytes 294920 | tf_op jit(solution)/shard_map/ppermute | solution.py:26
  12.6 5.6 %collective-permute-start.7 = (bf16[64,1280]{1,0:T(8,128)(2,1)S(1)}, bf16[64,1280]{1,0:T(8,128)(2,1)S(1)}, u32[]{:S(2)}, u32[]{:S(2)}) collective-permute-start(bf16[64,1280]{1,0:T(8,128)(2,1)S(1)} %get-tuple-element.28), channel_id=1, source_target_pairs={{0,16},{1,9},{2,18},{3,11},{4,20},{5,13},{6,22},{7,15},{8,24},{9,1... | collective-permute-start | bytes 491528 | tf_op jit(solution)/shard_map/ppermute | solution.py:36
  15.9 14.9 %collective-permute-start.3 = (bf16[64,2048]{1,0:T(8,128)(2,1)S(1)}, bf16[64,2048]{1,0:T(8,128)(2,1)S(1)}, u32[]{:S(2)}, u32[]{:S(2)}) collective-permute-start(bf16[64,2048]{1,0:T(8,128)(2,1)S(1)} %get-tuple-element.24), channel_id=1, source_target_pairs={{0,16},{1,9},{2,18},{3,11},{4,20},{5,13},{6,22},{7,15},{8,24},{9,1... | collective-permute-start | bytes 786440 | tf_op jit(solution)/shard_map/ppermute | solution.py:36
  17.9 7.2 %collective-permute-start.9 = (bf16[64,768]{1,0:T(8,128)(2,1)S(1)}, bf16[64,768]{1,0:T(8,128)(2,1)S(1)}, u32[]{:S(2)}, u32[]{:S(2)}) collective-permute-start(bf16[64,768]{1,0:T(8,128)(2,1)S(1)} %shard_map.91), channel_id=1, source_target_pairs={{0,16},{1,9},{2,18},{3,11},{4,20},{5,13},{6,22},{7,15},{8,24},{9,1... | collective-permute-start | bytes 294920 | tf_op jit(solution)/shard_map/ppermute | solution.py:36
  18.3 12.5 %collective-permute-start.8 = (bf16[64,1280]{1,0:T(8,128)(2,1)S(1)}, bf16[64,1280]{1,0:T(8,128)(2,1)S(1)}, u32[]{:S(2)}, u32[]{:S(2)}) collective-permute-start(bf16[64,1280]{1,0:T(8,128)(2,1)S(1)} %shard_map.90), channel_id=1, source_target_pairs={{0,8},{1,17},{2,10},{3,19},{4,12},{5,21},{6,14},{7,23},{8,0},{9,25... | collective-permute-start | bytes 491528 | tf_op jit(solution)/shard_map/ppermute | solution.py:36
  25.2 5.6 %collective-permute-start.10 = (bf16[64,768]{1,0:T(8,128)(2,1)S(1)}, bf16[64,768]{1,0:T(8,128)(2,1)S(1)}, u32[]{:S(2)}, u32[]{:S(2)}) collective-permute-start(bf16[64,768]{1,0:T(8,128)(2,1)S(1)} %shard_map.92), channel_id=1, source_target_pairs={{0,8},{1,17},{2,10},{3,19},{4,12},{5,21},{6,14},{7,23},{8,0},{9,25... | collective-permute-start | bytes 294920 | tf_op jit(solution)/shard_map/ppermute | solution.py:36
  31.0 1.2 %collective-permute-start.11 = (f32[2,64]{1,0:T(2,128)S(1)}, f32[2,64]{1,0:T(2,128)S(1)}, u32[]{:S(2)}, u32[]{:S(2)}) collective-permute-start(f32[2,64]{1,0:T(2,128)S(1)} %get-tuple-element.32), channel_id=1, source_target_pairs={{0,1},{1,0},{2,3},{3,2},{4,5},{5,4},{6,7},{7,6},{8,9},{9,8},{10,11... | collective-permute-start | bytes 1544 | tf_op jit(solution)/shard_map/ppermute | solution.py:41
  32.2 4.5 %collective-permute-start.13 = (f32[2,64]{1,0:T(2,128)S(1)}, f32[2,64]{1,0:T(2,128)S(1)}, u32[]{:S(2)}, u32[]{:S(2)}) collective-permute-start(f32[2,64]{1,0:T(2,128)S(1)} %pad_maximum_fusion), channel_id=1, source_target_pairs={{0,4},{1,7},{2,6},{3,5},{4,0},{5,3},{6,2},{7,1},{8,12},{9,15},{10,... | collective-permute-start | bytes 1544 | tf_op jit(solution)/shard_map/ppermute | solution.py:41
  34.9 3.6 %collective-permute-start.12 = (f32[2,64]{1,0:T(2,128)S(1)}, f32[2,64]{1,0:T(2,128)S(1)}, u32[]{:S(2)}, u32[]{:S(2)}) collective-permute-start(f32[2,64]{1,0:T(2,128)S(1)} %pad_maximum_fusion), channel_id=1, source_target_pairs={{0,2},{1,3},{2,0},{3,1},{4,6},{5,7},{6,4},{7,5},{8,10},{9,11},{10,... | collective-permute-start | bytes 1544 | tf_op jit(solution)/shard_map/ppermute | solution.py:41
  36.8 1.7 %collective-permute-start.14 = (f32[2,64]{1,0:T(2,128)S(1)}, f32[2,64]{1,0:T(2,128)S(1)}, u32[]{:S(2)}, u32[]{:S(2)}) collective-permute-start(f32[2,64]{1,0:T(2,128)S(1)} %collective-permute-done.13), channel_id=1, source_target_pairs={{0,1},{1,0},{2,3},{3,2},{4,5},{5,4},{6,7},{7,6},{8,9},{9,8},{10,11... | collective-permute-start | bytes 1544 | tf_op jit(solution)/shard_map/ppermute | solution.py:41

commit v5 on v4

--- a/solution.py
+++ b/solution.py
@@ -120,14 +120,19 @@
             out[:, at : at + tile] = part[k * rows : (k + 1) * rows, :].astype(out.dtype)
 
 
-def first_kernel(tile, picks_ref, damage_ref, own, near, mated, side, weight, out):
+def early_kernel(picks_ref, own, near, weight):
     odd = lax.axis_index("node") % 2
-    total = jnp.dot(
+    weight[...] = jnp.dot(
         rows_of(own, lax.axis_index("grp") ^ 3, near.shape[0]),
         picks_ref[0],
         preferred_element_type=jnp.float32,
-    )
-    for ref, step in ((near, 2 + odd), (mated, 3 - odd), (side, 1)):
+    ) + jnp.dot(near[...], picks_ref[2 + odd], preferred_element_type=jnp.float32)
+
+
+def first_kernel(tile, picks_ref, damage_ref, early, mated, side, weight, out):
+    odd = lax.axis_index("node") % 2
+    total = early[...]
+    for ref, step in ((mated, 3 - odd), (side, 1)):
         total += jnp.dot(ref[...], picks_ref[step], preferred_element_type=jnp.float32)
     weight[...] = total.astype(weight.dtype)
     project(weight[...], damage_ref, 0, [out], tile)
@@ -272,9 +277,7 @@
         ],
         limit=32,
     )
-    picks = call(
-        functools.partial(picks_kernel, groups), [((groups, rows, slots), half)], [FULL], named
-    )[0]
+    picks = call(functools.partial(picks_kernel, groups), [((groups, rows, slots), half)], [FULL], named)[0]
     part = ((per_group, cells), half)
 
     if paired:
@@ -288,18 +291,17 @@
         near_tail = split_swap(near_tail, (2, 3))
         heads = (near_head, swap(near_head, "node", 1), side_head)
         tails = (near_tail, swap(near_tail, "node", 1), side_tail)
+        early = call(early_kernel, [((per_group, slots), full)], [FULL] * 3, picks, scores, near_head)[0]
         weight, first = call(
             functools.partial(first_kernel, tile),
             [((per_group, slots), half), (pieces[0], half)],
-            [FULL] * 6,
+            [FULL] * 5,
             picks,
             damage,
-            scores,
-            *heads,
+            early,
+            *heads[1:],
         )
-        second = call(
-            functools.partial(second_kernel, tile), [(pieces[1], half)], [FULL] * 2, weight, damage
-        )[0]
+        second = call(functools.partial(second_kernel, tile), [(pieces[1], half)], [FULL] * 2, weight, damage)[0]
         passed = [split_swap(x, (2, 1)) for x in (first, second)]
         sent, *kept, weight = call(
             functools.partial(other_kernel, tile),
@@ -315,9 +317,7 @@
         for k in range(2):
             both = call(add_kernel, [(pieces[k], half)], [FULL] * 2, kept[k], passed[k])[0]
             arrived.append(split_swap(both, (1, 2)))
-        own = call(
-            functools.partial(own_kernel, tile), [((per_group, cells), full)], [FULL] * 2, weight, damage
-        )[0]
+        own = call(functools.partial(own_kernel, tile), [((per_group, cells), full)], [FULL] * 2, weight, damage)[0]
     else:
         every = [scores] + [swap(scores, "grp", step) for step in range(1, groups)]
         own, *parts = call(
@@ -333,11 +333,7 @@
         arrived = [swap(x, "grp", step) for step, x in enumerate(parts, 1)]
 
     values, stats = call(
-        values_kernel,
-        [((per_group, cells), full), ((2, per_group), full)],
-        [FULL] * (1 + len(arrived)),
-        own,
-        *arrived,
+        values_kernel, [((per_group, cells), full), ((2, per_group), full)], [FULL] * (1 + len(arrived)), own, *arrived
     )
     surrogate = call(round_kernel, [part], [FULL], values)[0]
     squares, peak = over_nodes(stats, nodes)

time: 39.2 us -> 39.2 us (level)
    pallas_call x10 -> x11, Pallas kernels: 4.78 us -> 4.84 us  [call(): pl.pallas_call(kernel, out_shape=[jax.ShapeDtypeStruct(shape, kind) for s...]
where the time goes in v5:
time: 39.2 us; the launch traced here: 39 us
  starting transfers between devices  20.6 us (53%)
  waiting for transfers between devices  12.3 us (31%)
  Pallas kernels  4.84 us (12%)
  between operations  0.71 us (2%)
  other arithmetic  0.54 us (1%)
    ppermute x7, starting transfers between devices, split_swap(): return lax.ppermute(value, ('grp', 'node'), pairs)  12.1 us
    ppermute x7, waiting for transfers between devices, split_swap(): return lax.ppermute(value, ('grp', 'node'), pairs)  8.93 us
    pallas_call x11, Pallas kernels, call(): pl.pallas_call(kernel, out_shape=[jax.ShapeDtypeStruct(shape, kind) for s...  4.84 us
    ppermute x4, starting transfers between devices, node_swap(): return lax.ppermute(value, 'node', pairs)  4.26 us
    ppermute x4, starting transfers between devices, swap(): lax.ppermute(value, axis, [(i, mate(i, step, size)) for i in range(size)])  4.24 us
    ppermute x4, waiting for transfers between devices, node_swap(): return lax.ppermute(value, 'node', pairs)  2.41 us
    ppermute x4, waiting for transfers between devices, swap(): lax.ppermute(value, axis, [(i, mate(i, step, size)) for i in range(size)])  0.93 us
  transfers between devices with their start and end apart: 15, of which 7 were waited for; matrix products, arithmetic and copies ran while one was open for 0% of the time, Pallas kernels for 7%

profile of v5, /device:TPU:0, one launch (start us, length us, event | category | flops | bytes accessed | tf_op | source)
XLA Modules:
  0.0 39.0 jit_solution(14981316686698567714)
XLA Ops:
  0.6 1.9 %shard_map.85 = (bf16[256,256]{1,0:T(8,128)(2,1)S(1)}, s32[1,256]{1,0:T(1,128)S(1)}, bf16[256,2048]{1,0:T(8,128)(2,1)S(1)}, bf16[64,256]{1,0:T(8,128)(2,1)S(1)},...) custom-call(bf16[512,512]{1,0:T(8,128)(2,1)} %table_ref.1, ...), custom_call_target="tpu_custom_call" | custom-call | flops 1048576 | bytes 1048576 | tf_op jit(solution)/shard_map/pallas_call | solution.py:240
  2.6 3.1 %collective-permute-start = (bf16[192,256]{1,0:T(8,128)(2,1)S(1)}, bf16[192,256]{1,0:T(8,128)(2,1)S(1)}, u32[]{:S(2)}, u32[]{:S(2)}) collective-permute-start(bf16[192,256]{1,0:T(8,128)(2,1)S(1)} %get-tuple-element.21), channel_id=1, source_target_pairs={{0,16},{1,25},{2,18},{3,27},{4,20},{5,29},{6,22},{7,31},{8,24},{9,... | collective-permute-start | bytes 294920 | tf_op jit(solution)/shard_map/ppermute | solution.py:36
  5.6 0.1 collective-permute-start.4
  5.7 1.9 %collective-permute-start.6 = (bf16[64,256]{1,0:T(8,128)(2,1)S(1)}, bf16[64,256]{1,0:T(8,128)(2,1)S(1)}, u32[]{:S(2)}, u32[]{:S(2)}) collective-permute-start(bf16[64,256]{1,0:T(8,128)(2,1)S(1)} %get-tuple-element.27), channel_id=1, source_target_pairs={{0,8},{8,0},{16,24},{24,16},{1,9},{9,1},{17,25},{25,17},{2,10},{10... | collective-permute-start | bytes 98312 | tf_op jit(solution)/shard_map/ppermute | solution.py:26
  7.6 2.0 %collective-permute-done.4.near = bf16[64,256]{1,0:T(8,128)(2,1)S(1)} collective-permute-done((bf16[64,256]{1,0:T(8,128)(2,1)S(1)}, bf16[64,256]{1,0:T(8,128)(2,1)S(1)}, u32[]{:S(2)}, u32[]{:S(2)}) %collective-permute-start.4) | collective-permute-done | bytes 32800 | tf_op jit(solution)/shard_map/ppermute | solution.py:36
  9.6 0.2 collective-permute-start.5
  9.8 1.9 %collective-permute-start.2 = (bf16[192,256]{1,0:T(8,128)(2,1)S(1)}, bf16[192,256]{1,0:T(8,128)(2,1)S(1)}, u32[]{:S(2)}, u32[]{:S(2)}) collective-permute-start(bf16[192,256]{1,0:T(8,128)(2,1)S(1)} %get-tuple-element.22), channel_id=1, source_target_pairs={{0,8},{8,0},{16,24},{24,16},{1,9},{9,1},{17,25},{25,17},{2,10},{10... | collective-permute-start | bytes 294920 | tf_op jit(solution)/shard_map/ppermute | solution.py:26
  11.7 0.0 collective-permute-done.near
  11.7 0.2 collective-permute-start.1
  12.0 0.1 shard_map.86.picks_ref
  12.1 0.2 shard_map.89.early
  12.2 0.0 collective-permute-done.6.side
  12.3 0.0 collective-permute-done.5.mated
  12.3 0.4 %shard_map.90 = (bf16[64,256]{1,0:T(8,128)(2,1)S(1)}, bf16[64,1280]{1,0:T(8,128)(2,1)S(1)}) custom-call(bf16[4,256,256]{2,1,0:T(8,128)(2,1)S(1)} %shard_map.86.picks_ref, bf16[256,2048]{1,0:T(8,128)(2,1)S(1)} %get-tuple-element.19.damage_ref, f32[64,256]{1,0:T(8,128)S(1)} %shard_map.89.early, bf16[64,256]{1,0:T(8,128)(2,1)S(1)} %collective-permute-done.5.mated, ...), custom_call_target="tpu_custom_call" | custom-call | flops 1048576 | bytes 1048576 | tf_op jit(solution)/shard_map/pallas_call | solution.py:240
  12.7 1.6 %collective-permute-start.7 = (bf16[64,1280]{1,0:T(8,128)(2,1)S(1)}, bf16[64,1280]{1,0:T(8,128)(2,1)S(1)}, u32[]{:S(2)}, u32[]{:S(2)}) collective-permute-start(bf16[64,1280]{1,0:T(8,128)(2,1)S(1)} %get-tuple-element.28), channel_id=1, source_target_pairs={{0,16},{1,9},{2,18},{3,11},{4,20},{5,13},{6,22},{7,15},{8,24},{9,1... | collective-permute-start | bytes 491528 | tf_op jit(solution)/shard_map/ppermute | solution.py:36
  14.3 0.9 %collective-permute-done.2.side = bf16[192,256]{1,0:T(8,128)(2,1)S(1)} collective-permute-done((bf16[192,256]{1,0:T(8,128)(2,1)S(1)}, bf16[192,256]{1,0:T(8,128)(2,1)S(1)}, u32[]{:S(2)}, u32[]{:S(2)}) %collective-permute-start.2) | collective-permute-done | bytes 98336 | tf_op jit(solution)/shard_map/ppermute | solution.py:26
  15.2 0.0 collective-permute-done.1.mated
  15.2 0.7 %shard_map.87 = (bf16[64,2048]{1,0:T(8,128)(2,1)S(1)}, f32[64,1280]{1,0:T(8,128)S(1)}, f32[64,768]{1,0:T(8,128)S(1)}, bf16[64,256]{1,0:T(8,128)(2,1)S(1)}) custom-call(bf16[4,256,256]{2,1,0:T(8,128)(2,1)S(1)} %shard_map.86.picks_ref, bf16[256,2048]{1,0:T(8,128)(2,1)S(1)} %get-tuple-element.19.damage_ref, bf16[256,256]{1,0:T(8,128)(2,1)S(1)} %get-tuple-element.20.own, ...), custom_call_target="tpu_custom_call" | custom-call | flops 1048576 | bytes 1048576 | tf_op jit(solution)/shard_map/pallas_call | solution.py:240
  15.9 1.8 %collective-permute-start.3 = (bf16[64,2048]{1,0:T(8,128)(2,1)S(1)}, bf16[64,2048]{1,0:T(8,128)(2,1)S(1)}, u32[]{:S(2)}, u32[]{:S(2)}) collective-permute-start(bf16[64,2048]{1,0:T(8,128)(2,1)S(1)} %get-tuple-element.24), channel_id=1, source_target_pairs={{0,16},{1,9},{2,18},{3,11},{4,20},{5,13},{6,22},{7,15},{8,24},{9,1... | collective-permute-start | bytes 786440 | tf_op jit(solution)/shard_map/ppermute | solution.py:36
  17.7 0.2 shard_map.92
  17.9 0.3 collective-permute-start.9
  18.2 0.0 collective-permute-done.7.two_ref
  18.3 2.3 %collective-permute-start.8 = (bf16[64,1280]{1,0:T(8,128)(2,1)S(1)}, bf16[64,1280]{1,0:T(8,128)(2,1)S(1)}, u32[]{:S(2)}, u32[]{:S(2)}) collective-permute-start(bf16[64,1280]{1,0:T(8,128)(2,1)S(1)} %shard_map.91), channel_id=1, source_target_pairs={{0,8},{1,17},{2,10},{3,19},{4,12},{5,21},{6,14},{7,23},{8,0},{9,25... | collective-permute-start | bytes 491528 | tf_op jit(solution)/shard_map/ppermute | solution.py:36
  20.5 4.6 %collective-permute-done.9.two_ref = bf16[64,768]{1,0:T(8,128)(2,1)S(1)} collective-permute-done((bf16[64,768]{1,0:T(8,128)(2,1)S(1)}, bf16[64,768]{1,0:T(8,128)(2,1)S(1)}, u32[]{:S(2)}, u32[]{:S(2)}) %collective-permute-start.9) | collective-permute-done | bytes 98336 | tf_op jit(solution)/shard_map/ppermute | solution.py:36
  25.2 3.0 %collective-permute-start.10 = (bf16[64,768]{1,0:T(8,128)(2,1)S(1)}, bf16[64,768]{1,0:T(8,128)(2,1)S(1)}, u32[]{:S(2)}, u32[]{:S(2)}) collective-permute-start(bf16[64,768]{1,0:T(8,128)(2,1)S(1)} %shard_map.93), channel_id=1, source_target_pairs={{0,8},{1,17},{2,10},{3,19},{4,12},{5,21},{6,14},{7,23},{8,0},{9,25... | collective-permute-start | bytes 294920 | tf_op jit(solution)/shard_map/ppermute | solution.py:36
  28.2 0.3 shard_map.88.own_ref
  28.5 2.3 %collective-permute-done.10.refs_2_ = bf16[64,768]{1,0:T(8,128)(2,1)S(1)} collective-permute-done((bf16[64,768]{1,0:T(8,128)(2,1)S(1)}, bf16[64,768]{1,0:T(8,128)(2,1)S(1)}, u32[]{:S(2)}, u32[]{:S(2)}) %collective-permute-start.10) | collective-permute-done | bytes 98336 | tf_op jit(solution)/shard_map/ppermute | solution.py:36
  30.8 0.0 collective-permute-done.8.refs_1_
  30.8 0.0 collective-permute-done.3.refs_0_
  30.8 0.3 shard_map.94
  31.0 0.0 collective-permute-start.11
  31.1 1.1 %collective-permute-done.11 = f32[2,64]{1,0:T(2,128)S(1)} collective-permute-done((f32[2,64]{1,0:T(2,128)S(1)}, f32[2,64]{1,0:T(2,128)S(1)}, u32[]{:S(2)}, u32[]{:S(2)}) %collective-permute-start.11) | collective-permute-done | bytes 544 | tf_op jit(solution)/shard_map/ppermute | solution.py:41
  32.2 2.7 %collective-permute-start.13 = (f32[2,64]{1,0:T(2,128)S(1)}, f32[2,64]{1,0:T(2,128)S(1)}, u32[]{:S(2)}, u32[]{:S(2)}) collective-permute-start(f32[2,64]{1,0:T(2,128)S(1)} %pad_maximum_fusion), channel_id=1, source_target_pairs={{0,4},{1,7},{2,6},{3,5},{4,0},{5,3},{6,2},{7,1},{8,12},{9,15},{10,... | collective-permute-start | bytes 1544 | tf_op jit(solution)/shard_map/ppermute | solution.py:41
  34.9 1.6 %collective-permute-start.12 = (f32[2,64]{1,0:T(2,128)S(1)}, f32[2,64]{1,0:T(2,128)S(1)}, u32[]{:S(2)}, u32[]{:S(2)}) collective-permute-start(f32[2,64]{1,0:T(2,128)S(1)} %pad_maximum_fusion), channel_id=1, source_target_pairs={{0,2},{1,3},{2,0},{3,1},{4,6},{5,7},{6,4},{7,5},{8,10},{9,11},{10,... | collective-permute-start | bytes 1544 | tf_op jit(solution)/shard_map/ppermute | solution.py:41
  36.5 0.3 collective-permute-done.13
  36.8 0.0 collective-permute-start.14
  36.8 0.7 %shard_map.95 = bf16[64,2048]{1,0:T(8,128)(2,1)} custom-call(f32[64,2048]{1,0:T(8,128)S(1)} %get-tuple-element.31.values_ref), custom_call_target="tpu_custom_call" | custom-call | flops 1048576 | bytes 1048576 | tf_op jit(solution)/shard_map/pallas_call | solution.py:240
  37.5 1.0 %collective-permute-done.12 = f32[2,64]{1,0:T(2,128)S(1)} collective-permute-done((f32[2,64]{1,0:T(2,128)S(1)}, f32[2,64]{1,0:T(2,128)S(1)}, u32[]{:S(2)}, u32[]{:S(2)}) %collective-permute-start.12) | collective-permute-done | bytes 544 | tf_op jit(solution)/shard_map/ppermute | solution.py:41
  38.5 0.0 collective-permute-done.14
  38.5 0.5 %sqrt_bitcast_fusion = (f32[64]{0:T(128)}, f32[64]{0:T(128)}) fusion(f32[2,64]{1,0:T(2,128)S(1)} %collective-permute-done.14, f32[2,64]{1,0:T(2,128)S(1)} %collective-permute-done.13, f32[1,64]{1,0:T(1,128)S(1)} %get-tuple-element.35, f32[2,64]{1,0:T(2,128)S(1)} %collective-permute-done.12, f32[1,64]{1,0:T(1,128)S(1)} %get-tuple-element.36), kind=kLoop, calls=%fused_computation.1 | loop fusion | flops 512 | bytes 2560 | tf_op jit(solution)/shard_map/sqrt | solution.py:340
  (4 shorter events, 0.1 us)
Async XLA Ops:
  2.6 9.2 %collective-permute-start = (bf16[192,256]{1,0:T(8,128)(2,1)S(1)}, bf16[192,256]{1,0:T(8,128)(2,1)S(1)}, u32[]{:S(2)}, u32[]{:S(2)}) collective-permute-start(bf16[192,256]{1,0:T(8,128)(2,1)S(1)} %get-tuple-element.21), channel_id=1, source_target_pairs={{0,16},{1,25},{2,18},{3,27},{4,20},{5,29},{6,22},{7,31},{8,24},{9,... | collective-permute-start | bytes 294920 | tf_op jit(solution)/shard_map/ppermute | solution.py:36
  5.6 4.0 %collective-permute-start.4 = (bf16[64,256]{1,0:T(8,128)(2,1)S(1)}, bf16[64,256]{1,0:T(8,128)(2,1)S(1)}, u32[]{:S(2)}, u32[]{:S(2)}) collective-permute-start(bf16[64,256]{1,0:T(8,128)(2,1)S(1)} %get-tuple-element.26), channel_id=1, source_target_pairs={{0,16},{1,25},{2,18},{3,27},{4,20},{5,29},{6,22},{7,31},{8,24},{9,... | collective-permute-start | bytes 98312 | tf_op jit(solution)/shard_map/ppermute | solution.py:36
  5.7 6.5 %collective-permute-start.6 = (bf16[64,256]{1,0:T(8,128)(2,1)S(1)}, bf16[64,256]{1,0:T(8,128)(2,1)S(1)}, u32[]{:S(2)}, u32[]{:S(2)}) collective-permute-start(bf16[64,256]{1,0:T(8,128)(2,1)S(1)} %get-tuple-element.27), channel_id=1, source_target_pairs={{0,8},{8,0},{16,24},{24,16},{1,9},{9,1},{17,25},{25,17},{2,10},{10... | collective-permute-start | bytes 98312 | tf_op jit(solution)/shard_map/ppermute | solution.py:26
  9.6 2.6 %collective-permute-start.5 = (bf16[64,256]{1,0:T(8,128)(2,1)S(1)}, bf16[64,256]{1,0:T(8,128)(2,1)S(1)}, u32[]{:S(2)}, u32[]{:S(2)}) collective-permute-start(bf16[64,256]{1,0:T(8,128)(2,1)S(1)} %collective-permute-done.4.near), channel_id=1, source_target_pairs={{0,1},{1,0},{2,3},{3,2},{4,5},{5,4},{6,7},{7,6},{8,9},{9,8},{10,11... | collective-permute-start | bytes 98312 | tf_op jit(solution)/shard_map/ppermute | solution.py:26
  9.8 5.4 %collective-permute-start.2 = (bf16[192,256]{1,0:T(8,128)(2,1)S(1)}, bf16[192,256]{1,0:T(8,128)(2,1)S(1)}, u32[]{:S(2)}, u32[]{:S(2)}) collective-permute-start(bf16[192,256]{1,0:T(8,128)(2,1)S(1)} %get-tuple-element.22), channel_id=1, source_target_pairs={{0,8},{8,0},{16,24},{24,16},{1,9},{9,1},{17,25},{25,17},{2,10},{10... | collective-permute-start | bytes 294920 | tf_op jit(solution)/shard_map/ppermute | solution.py:26
  11.7 3.5 %collective-permute-start.1 = (bf16[192,256]{1,0:T(8,128)(2,1)S(1)}, bf16[192,256]{1,0:T(8,128)(2,1)S(1)}, u32[]{:S(2)}, u32[]{:S(2)}) collective-permute-start(bf16[192,256]{1,0:T(8,128)(2,1)S(1)} %collective-permute-done.near), channel_id=1, source_target_pairs={{0,1},{1,0},{2,3},{3,2},{4,5},{5,4},{6,7},{7,6},{8,9},{9,8},{10,11... | collective-permute-start | bytes 294920 | tf_op jit(solution)/shard_map/ppermute | solution.py:26
  12.7 5.5 %collective-permute-start.7 = (bf16[64,1280]{1,0:T(8,128)(2,1)S(1)}, bf16[64,1280]{1,0:T(8,128)(2,1)S(1)}, u32[]{:S(2)}, u32[]{:S(2)}) collective-permute-start(bf16[64,1280]{1,0:T(8,128)(2,1)S(1)} %get-tuple-element.28), channel_id=1, source_target_pairs={{0,16},{1,9},{2,18},{3,11},{4,20},{5,13},{6,22},{7,15},{8,24},{9,1... | collective-permute-start | bytes 491528 | tf_op jit(solution)/shard_map/ppermute | solution.py:36
  15.9 14.9 %collective-permute-start.3 = (bf16[64,2048]{1,0:T(8,128)(2,1)S(1)}, bf16[64,2048]{1,0:T(8,128)(2,1)S(1)}, u32[]{:S(2)}, u32[]{:S(2)}) collective-permute-start(bf16[64,2048]{1,0:T(8,128)(2,1)S(1)} %get-tuple-element.24), channel_id=1, source_target_pairs={{0,16},{1,9},{2,18},{3,11},{4,20},{5,13},{6,22},{7,15},{8,24},{9,1... | collective-permute-start | bytes 786440 | tf_op jit(solution)/shard_map/ppermute | solution.py:36
  17.9 7.2 %collective-permute-start.9 = (bf16[64,768]{1,0:T(8,128)(2,1)S(1)}, bf16[64,768]{1,0:T(8,128)(2,1)S(1)}, u32[]{:S(2)}, u32[]{:S(2)}) collective-permute-start(bf16[64,768]{1,0:T(8,128)(2,1)S(1)} %shard_map.92), channel_id=1, source_target_pairs={{0,16},{1,9},{2,18},{3,11},{4,20},{5,13},{6,22},{7,15},{8,24},{9,1... | collective-permute-start | bytes 294920 | tf_op jit(solution)/shard_map/ppermute | solution.py:36
  18.3 12.5 %collective-permute-start.8 = (bf16[64,1280]{1,0:T(8,128)(2,1)S(1)}, bf16[64,1280]{1,0:T(8,128)(2,1)S(1)}, u32[]{:S(2)}, u32[]{:S(2)}) collective-permute-start(bf16[64,1280]{1,0:T(8,128)(2,1)S(1)} %shard_map.91), channel_id=1, source_target_pairs={{0,8},{1,17},{2,10},{3,19},{4,12},{5,21},{6,14},{7,23},{8,0},{9,25... | collective-permute-start | bytes 491528 | tf_op jit(solution)/shard_map/ppermute | solution.py:36
  25.2 5.6 %collective-permute-start.10 = (bf16[64,768]{1,0:T(8,128)(2,1)S(1)}, bf16[64,768]{1,0:T(8,128)(2,1)S(1)}, u32[]{:S(2)}, u32[]{:S(2)}) collective-permute-start(bf16[64,768]{1,0:T(8,128)(2,1)S(1)} %shard_map.93), channel_id=1, source_target_pairs={{0,8},{1,17},{2,10},{3,19},{4,12},{5,21},{6,14},{7,23},{8,0},{9,25... | collective-permute-start | bytes 294920 | tf_op jit(solution)/shard_map/ppermute | solution.py:36
  31.0 1.2 %collective-permute-start.11 = (f32[2,64]{1,0:T(2,128)S(1)}, f32[2,64]{1,0:T(2,128)S(1)}, u32[]{:S(2)}, u32[]{:S(2)}) collective-permute-start(f32[2,64]{1,0:T(2,128)S(1)} %get-tuple-element.32), channel_id=1, source_target_pairs={{0,1},{1,0},{2,3},{3,2},{4,5},{5,4},{6,7},{7,6},{8,9},{9,8},{10,11... | collective-permute-start | bytes 1544 | tf_op jit(solution)/shard_map/ppermute | solution.py:41
  32.2 4.5 %collective-permute-start.13 = (f32[2,64]{1,0:T(2,128)S(1)}, f32[2,64]{1,0:T(2,128)S(1)}, u32[]{:S(2)}, u32[]{:S(2)}) collective-permute-start(f32[2,64]{1,0:T(2,128)S(1)} %pad_maximum_fusion), channel_id=1, source_target_pairs={{0,4},{1,7},{2,6},{3,5},{4,0},{5,3},{6,2},{7,1},{8,12},{9,15},{10,... | collective-permute-start | bytes 1544 | tf_op jit(solution)/shard_map/ppermute | solution.py:41
  34.9 3.6 %collective-permute-start.12 = (f32[2,64]{1,0:T(2,128)S(1)}, f32[2,64]{1,0:T(2,128)S(1)}, u32[]{:S(2)}, u32[]{:S(2)}) collective-permute-start(f32[2,64]{1,0:T(2,128)S(1)} %pad_maximum_fusion), channel_id=1, source_target_pairs={{0,2},{1,3},{2,0},{3,1},{4,6},{5,7},{6,4},{7,5},{8,10},{9,11},{10,... | collective-permute-start | bytes 1544 | tf_op jit(solution)/shard_map/ppermute | solution.py:41
  36.8 1.7 %collective-permute-start.14 = (f32[2,64]{1,0:T(2,128)S(1)}, f32[2,64]{1,0:T(2,128)S(1)}, u32[]{:S(2)}, u32[]{:S(2)}) collective-permute-start(f32[2,64]{1,0:T(2,128)S(1)} %collective-permute-done.13), channel_id=1, source_target_pairs={{0,1},{1,0},{2,3},{3,2},{4,5},{5,4},{6,7},{7,6},{8,9},{9,8},{10,11... | collective-permute-start | bytes 1544 | tf_op jit(solution)/shard_map/ppermute | solution.py:41
